TPU v7x, 32 devices: a 4x4x1 block of a 4x4x8 slice. The times are simulated.
32 devices in a mesh: dp: 1 (over z), tp: 32 (over x, y, core).
Axes of the slice: x: 4, y: 4, z: 1, core: 2. Of those that a mesh axis runs over, the one named last changes fastest.
The devices are a block of a 4x4x8 slice.
Arguments:
- x: bfloat16 [4096, 8192], P(('dp', 'tp'))
- dy: bfloat16 [4096, 8192], P(('dp', 'tp'))
- pre: bfloat16 [4096, 32768], P('dp', 'tp')
- w_in: bfloat16 [8192, 32768], P(None, 'tp')
- w_down: bfloat16 [32768, 8192], P('tp')
Outputs:
- output 1: bfloat16 [4096, 8192], P(('dp', 'tp'))
- output 2: bfloat16 [8192, 32768], P('dp', 'tp')
- output 3: bfloat16 [32768, 8192], P(('dp', 'tp'))
All inputs are finite; a program needn't handle non-finite values.
Results may differ from a plain program's by a relative error of at most 0.012.
Values are sent between devices in bfloat16 or wider.
A program may use at most 768 MiB of HBM per device.

v0:
```python
import jax
import jax.numpy as jnp


def act(pre):
    return jax.nn.gelu(pre)


def solution(mesh):
    def step(x, dy, pre, w_in, w_down):
        hidden, back = jax.vjp(act, pre.astype(jnp.float32))
        d_hidden = jnp.dot(dy, w_down.T, preferred_element_type=jnp.float32)
        d_pre = back(d_hidden)[0].astype(jnp.bfloat16)
        dx = jnp.dot(d_pre, w_in.T)
        groups = mesh.shape["dp"]

        def by_group(a, b):
            a, b = (t.reshape(groups, -1, t.shape[-1]) for t in (a, b))
            product = jnp.einsum("gta,gtb->gab", a, b, preferred_element_type=jnp.float32)
            return product.astype(jnp.bfloat16).reshape(-1, b.shape[-1])

        return dx, by_group(x, d_pre), by_group(hidden.astype(jnp.bfloat16), dy)

    return step
```

profile of v0, /device:TPU:97, one launch (start us, length us, event | category | flops | bytes accessed | tf_op | source)
XLA Modules:
  0.0 701.1 jit_solution(10939539064742759199)
XLA Ops:
  7.2 0.1 all-gather.7.cloned.1.call-start
  7.2 0.7 all-gather.7.cloned.1.call-update
  8.0 0.1 all-gather.9.cloned.1.call-start
  8.0 0.7 all-gather.9.cloned.1.call-update
  8.8 0.1 reduce-scatter.5.cloned.1.call-start
  8.9 201.4 %all-gather.7.cloned.1.call-done = bf16[4096,8192]{1,0:T(8,128)(2,1)} async-done(((bf16[128,8192]{1,0:T(8,128)(2,1)}), bf16[4096,8192]{1,0:T(8,128)(2,1)}) %all-gather.7.cloned.1.call-update) | async-done | bytes 67108880 | tf_op args[1]
  210.2 79.5 %fusion.22 = f32[4096,1024]{1,0:T(8,128)} fusion(bf16[4096,8192]{1,0:T(8,128)(2,1)} %all-gather.7.cloned.1.call-done, bf16[1024,8192]{1,0:T(8,128)(2,1)} %param.1), kind=kOutput, calls=%fused_computation.26 | convolution fusion | flops 68719476736 | bytes 100663296 | tf_op jit(solution)/dot_general | solution.py:12
  289.8 95.8 %fusion.20 = bf16[4096,8192]{1,0:T(8,128)(2,1)} fusion(bf16[8192,1024]{1,0:T(8,128)(2,1)} %param.3, bf16[4096,1024]{1,0:T(8,128)(2,1)} %param.2, f32[4096,1024]{1,0:T(8,128)} %fusion.22), kind=kOutput, calls=%fused_computation.25 | convolution fusion | flops 68807557120 | bytes 109051904 | tf_op jit(solution)/dot_general | solution.py:14
  385.6 0.1 reduce-scatter.5.cloned.1.call-update
  385.6 16.6 %fusion.37 = bf16[4096,1024]{1,0:T(8,128)(2,1)} fusion(bf16[4096,1024]{1,0:T(8,128)(2,1)} %param.2, f32[4096,1024]{1,0:T(8,128)} %fusion.22), kind=kLoop, calls=%fused_computation.8.clone.clone.1 | loop fusion | flops 88080384 | bytes 33554432 | tf_op jit(solution)/gta,gtb->gab/dot_general | solution.py:19
  402.3 4.9 all-gather.9.cloned.1.call-done
  407.2 79.2 %convert_bitcast_fusion = bf16[8192,1024]{0,1:T(8,128)(2,1)} fusion(bf16[4096,8192]{1,0:T(8,128)(2,1)} %all-gather.9.cloned.1.call-done, bf16[4096,1024]{1,0:T(8,128)(2,1)} %fusion.37), kind=kOutput, calls=%fused_computation.15 | convolution fusion | flops 68727865344 | bytes 92274688 | tf_op jit(solution)/gta,gtb->gab/dot_general | solution.py:19
  486.4 22.4 %copy = bf16[8192,1024]{1,0:T(8,128)(2,1)} copy(bf16[8192,1024]{0,1:T(8,128)(2,1)} %convert_bitcast_fusion) | data formatting | bytes 33554432
  508.8 104.1 %convolution_convert_fusion = bf16[1024,8192]{1,0:T(8,128)(2,1)} fusion(bf16[4096,8192]{1,0:T(8,128)(2,1)} %all-gather.7.cloned.1.call-done, bf16[4096,1024]{1,0:T(8,128)(2,1)} %param.2), kind=kOutput, calls=%fused_computation.16 | convolution fusion | flops 68769808384 | bytes 92274688 | tf_op jit(solution)/gta,gtb->gab/dot_general | solution.py:19
  612.9 81.6 %reduce-scatter.5.cloned.1.call-done = bf16[128,8192]{1,0:T(8,128)(2,1)} async-done(((bf16[4096,8192]{1,0:T(8,128)(2,1)}), bf16[128,8192]{1,0:T(8,128)(2,1)}) %reduce-scatter.5.cloned.1.call-update) | async-done | bytes 2097168
Async XLA Ops:
  7.2 203.1 %all-gather.7.cloned.1.call-start = ((), (), s32[]{:S(2)}) async-start(), calls=%async_computation.1 | async-start | bytes 69206016 | tf_op args[1]
  8.0 399.2 %all-gather.9.cloned.1.call-start = ((), (), s32[]{:S(2)}) async-start(), calls=%async_computation.2 | async-start | bytes 69206016 | tf_op args[0]
  8.8 685.8 %reduce-scatter.5.cloned.1.call-start = ((), (), s32[]{:S(2)}) async-start(), calls=%async_computation.3 | async-start | bytes 69206016
Sparse Core Ops, SparseCore 0:
  10.1 200.1 all-gather.6
  212.3 194.8 all-gather.8
  411.6 282.8 reduce-scatter.4
where the time goes:
time: 702 us; the launch traced here: 701 us
  matrix products  359 us (51%)
  waiting for transfers between devices  289 us (41%)
  local copies, waits for them, and re-layouts  22.4 us (3%)
  other arithmetic  16.6 us (2%)
  between operations  13.8 us (2%)
    unnamed x6, waiting for transfers between devices  289 us
    dot_general x2, matrix products, by_group(): jnp.einsum('gta,gtb->gab', a, b, preferred_element_type=jnp.float32)  183 us
    dot_general x1, matrix products, step(): dx = jnp.dot(d_pre, w_in.T)  95.8 us
    dot_general x1, matrix products, step(): d_hidden = jnp.dot(dy, w_down.T, preferred_element_type=jnp.float32)  79.5 us
    unnamed x1, local copies, waits for them, and re-layouts  22.4 us
    dot_general x1, other arithmetic, by_group(): jnp.einsum('gta,gtb->gab', a, b, preferred_element_type=jnp.float32)  16.6 us
  transfers between devices with their start and end apart: 3, of which 3 were waited for; matrix products, arithmetic and copies ran while one was open for 57% of the time, Pallas kernels for 0%

commit v1 on v0

v1 whole, which is shorter than its diff:
```python
import functools
import math

import jax
import jax.numpy as jnp
from jax import lax
from jax.experimental import pallas as pl
from jax.experimental.pallas import tpu as pltpu
from jax.sharding import PartitionSpec as P

MESH = pl.DeviceIdType.MESH
F32, BF16 = jnp.float32, jnp.bfloat16
SUB = 4
TILE = 256


def ring_pos(side, chip, ring):
    a, b = chip // side, chip % side
    return jnp.where(ring == 0, a, b) * side + (a + b) % side


def ring_chip(side, pos, ring):
    pos = (pos + side * side) % (side * side)
    major = pos // side
    minor = (pos % side - major + side) % side
    return jnp.where(ring == 0, major * side + minor, minor * side + major)


def dot(a, b, ca, cb):
    return lax.dot_general(a, b, (((ca,), (cb,)), ((), ())), preferred_element_type=F32)


def gelu_and_slope(p):
    c = math.sqrt(2.0 / math.pi)
    sq = p * p
    t = jnp.tanh(c * (p + 0.044715 * (sq * p)))
    cdf = 0.5 * (1.0 + t)
    slope = cdf + p * (0.5 * (1.0 - t * t)) * (c * (1.0 + 3 * 0.044715 * sq))
    return p * cdf, slope


def kernel(n, x, dy, pre, w_in, w_down, dx, dw_in, dw_down, gb, rsb, sbb, dpre, w2,
           agr, ags, d2r, d2s, rsr, rss, sbr, sbs, wsem, psem, osem, lsem, tsem):
    S = n // 2
    side = math.isqrt(S)
    R, D = x.shape
    H, Q, F = R // 2, R // 2 // SUB, pre.shape[1]
    DC = D // SUB
    NT = D // TILE
    me = lax.axis_index("tp")
    chip, core = me // 2, me % 2
    pos, pos2 = ring_pos(side, chip, core), ring_pos(side, chip, 1 - core)
    nxt = [ring_chip(side, pos + 1, core) * 2 + core, ring_chip(side, pos - 1, core) * 2 + core]
    sib = chip * 2 + 1 - core

    def remote(src, dst, ssem, rsem, dev):
        return pltpu.make_async_remote_copy(src, dst, ssem, rsem, device_id={"tp": dev}, device_id_type=MESH)

    def land(v):
        return v + v // (S - 1)

    def ag_copy(v, d, q, src=None):
        rows = pl.ds(d * H + q * Q, Q)
        slot = jnp.where(v % (S - 1) == 0, land(v) + S - 1, land(v) - 1)
        src = gb.at[0, slot, rows] if src is None else src.at[rows]
        return remote(src, gb.at[0, land(v), rows], ags.at[v], agr.at[v, d, q], nxt[d])

    def pump(v, q, last=False):
        for d in range(2):
            ag_copy(v, d, q).wait_recv()
            if not last:
                ag_copy(v + 1, d, q).start()

    def d2d(w, src=None):
        return remote(gb.at[0, w] if src is None else src, gb.at[1, w], d2s.at[w], d2r.at[w], sib)

    bar = pltpu.get_barrier_semaphore()
    for dev in (*nxt, sib):
        pl.semaphore_signal(bar, inc=1, device_id={"tp": dev}, device_id_type=MESH)
    pl.semaphore_wait(bar, 3)
    for q in range(SUB):
        for d in range(2):
            ag_copy(0, d, q, dy).start()
    d2d(S - 1, dy).start()
    d2d(2 * S - 1, x).start()
    load_w2 = pltpu.make_async_copy(w_in, w2, wsem.at[1])

    def first(hT):
        def p1(w1, a, prb):
            load_w1 = pltpu.make_async_copy(w_down, w1, wsem.at[0])
            own = [pltpu.make_async_copy(dy, a.at[0], lsem.at[0]), pltpu.make_async_copy(x, a.at[1], lsem.at[1])]
            put = [pltpu.make_async_copy(a.at[0], gb.at[0, S - 1], lsem.at[0]),
                   pltpu.make_async_copy(a.at[1], gb.at[0, 2 * S - 1], lsem.at[1])]
            for c in own:
                c.start()
            load_w1.start()
            load_w2.start()
            for o, c in zip(own, put):
                o.wait()
                c.start()
            for c in put:
                c.wait()

            def loads(e):
                out = [pltpu.make_async_copy(gb.at[:, e], a, lsem.at[0])]
                for h, (ps, cr) in enumerate(((pos, core), (pos2, 1 - core))):
                    for d in range(2):
                        c = ring_chip(side, ps + (e + 1 if d else 2 * S - 1 - e), cr)
                        row = pl.multiple_of((c * 2 + cr) * R + d * H, H)
                        out.append(pltpu.make_async_copy(pre.at[pl.ds(row, H)], prb.at[h, pl.ds(d * H, H)], psem.at[h, d]))
                return out

            @pl.loop(0, S + 1)
            def _(v):
                @pl.when(v == 1)
                def _():
                    load_w1.wait()

                e = (v + S - 2) % S

                @pl.loop(0, SUB)
                def _(q):
                    pump(v, q)

                    @pl.when(v >= 1)
                    def _():
                        @pl.when(q == 0)
                        def _():
                            for c in loads(e):
                                c.wait()

                        FC = F // SUB
                        cols = pl.ds(pl.multiple_of(q * FC, FC), FC)
                        dh = dot(a[...].reshape(2 * R, D), w1[cols, :], 1, 1)
                        for h in range(2):
                            hid, slope = gelu_and_slope(prb[h, :, cols].astype(F32))
                            dpre[h, e, :, cols] = (dh[h * R : (h + 1) * R] * slope).astype(BF16)
                            tok = pl.ds(pl.multiple_of((h * S + e) * R, R), R)
                            hT[cols, tok] = hid.T.astype(BF16)

                d2d(land(v)).start()

                @pl.when(v < S)
                def _():
                    e1 = (v + S - 1) % S
                    d2d(e1).wait_recv()
                    for c in loads(e1):
                        c.start()

        pl.run_scoped(p1, pltpu.VMEM((F, D), BF16), pltpu.VMEM((2, R, D), BF16), pltpu.VMEM((2, R, F), BF16))

        def p2(tile, dout, sst):
            load_w2.wait()

            def tile_load(i):
                cols = pl.ds(pl.multiple_of(i * TILE, TILE), TILE)
                return pltpu.make_async_copy(gb.at[:, pl.ds(0, S), :, cols], tile.at[i % 2], tsem.at[i % 2])

            def tile_out(i):
                cols = pl.ds(pl.multiple_of(i * TILE, TILE), TILE)
                return pltpu.make_async_copy(dout.at[i % 2], dw_down.at[:, cols], osem.at[i % 2])

            def sib_copy(k, c):
                return remote(sst.at[k % 2, c], sbb.at[k, c], sbs.at[k % 2, c], sbr.at[k, c], sib)

            tile_load(0).start()

            @pl.loop(0, S)
            def _(g):
                def step(u):
                    v = S + 1 + u // SUB
                    pump(v, u % SUB)

                    @pl.when(u % SUB == SUB - 1)
                    def _():
                        d2d(land(v)).start()

                @pl.loop(0, 2)
                def _(j):
                    step(3 * g + j)
                    i = 2 * g + j
                    tile_load(i).wait()

                    @pl.when(i + 1 < NT)
                    def _():
                        tile_load(i + 1).start()

                    @pl.when(i >= 2)
                    def _():
                        tile_out(i - 2).wait()

                    dout[i % 2] = dot(hT[...], tile[i % 2].reshape(2 * S * R, TILE), 1, 0).astype(BF16)
                    tile_out(i).start()

                step(3 * g + 2)

                @pl.loop(0, 2)
                def _(j):
                    k, c = g // 2, (g % 2) * 2 + j

                    @pl.when(k >= 2)
                    def _():
                        sib_copy(k - 2, c).wait_send()

                    part = dot(dpre[1, pl.ds(2 * k, 2)].reshape(2 * R, F), w2[pl.ds(pl.multiple_of(c * DC, DC), DC), :], 1, 1)
                    sst[k % 2, c] = part.astype(BF16).reshape(2, R, DC)
                    sib_copy(k, c).start()

            for i in range(NT - 2, NT):
                tile_out(i).wait()

            @pl.loop(S // 2 - 2, S // 2)
            def _(k):
                for c in range(SUB):
                    sib_copy(k, c).wait_send()

        pl.run_scoped(p2, pltpu.VMEM((2, 2, S, R, TILE), BF16), pltpu.VMEM((2, F, TILE), BF16), pltpu.VMEM((2, SUB, 2, R, DC), BF16))

    pl.run_scoped(first, pltpu.VMEM((F, 2 * S * R), BF16))

    def p3(own, xt, eo, got, gsib, out):
        last = 2 * (S - 1) - 1

        def x_load(i):
            cols = pl.ds(pl.multiple_of(i * TILE, TILE), TILE)
            return pltpu.make_async_copy(gb.at[:, pl.ds(S, S), :, cols], xt.at[i % 2], tsem.at[i % 2])

        def e_out(i):
            return pltpu.make_async_copy(eo.at[i % 2], dw_in.at[pl.ds(pl.multiple_of(i * TILE, TILE), TILE)], osem.at[i % 2])

        def rs_copy(s, d, q):
            rows = pl.ds(d * H, H)
            return remote(out.at[s % 2, q, rows], rsb.at[s, q, rows], rss.at[s % 2, d, q], rsr.at[s, d, q], nxt[d])

        def got_load(s, q):
            return pltpu.make_async_copy(rsb.at[s - 1, q], got.at[q % 2], lsem.at[q % 2])

        def sib_load(s, q):
            return pltpu.make_async_copy(sbb.at[s // 2, q, s % 2], gsib.at[q % 2], psem.at[0, q % 2])

        def sib_arrive(s, q):
            @pl.when(s % 2 == 0)
            def _():
                remote(sbb.at[s // 2, q], sbb.at[s // 2, q], sbs.at[0, q], sbr.at[s // 2, q], sib).wait_recv()

        def dx_out(q):
            return pltpu.make_async_copy(out.at[(S - 1) % 2, q], dx.at[:, pl.ds(pl.multiple_of(q * DC, DC), DC)], tsem.at[2 + q])

        sib_arrive(0, 0)
        sib_load(0, 0).start()

        @pl.loop(0, S)
        def _(s):
            @pl.loop(0, SUB)
            def _(q):
                @pl.when(s % 2 == 0)
                def _():
                    part = dot(dpre[0, pl.ds(s, 2)].reshape(2 * R, F), w2[pl.ds(pl.multiple_of(q * DC, DC), DC), :], 1, 1)
                    own[q] = part.reshape(2, R, DC)

                @pl.when(s >= 2)
                def _():
                    for d in range(2):
                        rs_copy(s - 2, d, q).wait_send()

                sib_load(s, q).wait()

                @pl.when(s == 0)
                def _():
                    out[s % 2, q] = (own[q, s % 2] + gsib[q % 2].astype(F32)).astype(BF16)

                @pl.when(s > 0)
                def _():
                    got_load(s, q).wait()
                    out[s % 2, q] = (own[q, s % 2] + gsib[q % 2].astype(F32) + got[q % 2].astype(F32)).astype(BF16)

                @pl.when(s < S - 1)
                def _():
                    for d in range(2):
                        rs_copy(s, d, q).start()

                @pl.when(s == S - 1)
                def _():
                    dx_out(q).start()

                @pl.when(s == 0)
                def _():
                    pump(last, q, True)

                @pl.when((s == 0) & (q == SUB - 1))
                def _():
                    d2d(land(last)).start()

                @pl.when((s < S - 1) | (q < SUB - 1))
                def _():
                    q1 = (q + 1) % SUB
                    s1 = s + (q + 1) // SUB
                    sib_arrive(s1, q1)
                    sib_load(s1, q1).start()

                    @pl.when(s1 > 0)
                    def _():
                        for d in range(2):
                            rs_copy(s1 - 1, d, q1).wait_recv()
                        got_load(s1, q1).start()

                @pl.when(s % 2 == 1)
                def _():
                    i = (s // 2) * SUB + q

                    @pl.when(i == 0)
                    def _():
                        @pl.loop(S, 2 * S)
                        def _(w):
                            d2d(w).wait_recv()

                        x_load(0).start()

                    x_load(i).wait()

                    @pl.when(i + 1 < NT)
                    def _():
                        x_load(i + 1).start()

                    @pl.when(i >= 2)
                    def _():
                        e_out(i - 2).wait()

                    eo[i % 2] = dot(xt[i % 2].reshape(2 * S * R, TILE), dpre[...].reshape(2 * S * R, F), 0, 0).astype(BF16)
                    e_out(i).start()

        for i in range(NT - 2, NT):
            e_out(i).wait()
        for q in range(SUB):
            for d in range(2):
                rs_copy(S - 2, d, q).wait_send()
            dx_out(q).wait()

    pl.run_scoped(p3, pltpu.VMEM((SUB, 2, R, DC), F32), pltpu.VMEM((2, 2, S, R, TILE), BF16), pltpu.VMEM((2, TILE, F), BF16),
                  pltpu.VMEM((2, R, DC), BF16), pltpu.VMEM((2, R, DC), BF16), pltpu.VMEM((2, SUB, R, DC), BF16))

    @pl.loop(0, 2 * (S - 1))
    def _(v):
        remote(gb.at[0, 0], gb.at[0, 0], ags.at[v], agr.at[v, 0, 0], nxt[0]).wait_send()

    @pl.loop(0, 2 * S)
    def _(w):
        d2d(w).wait_send()


def solution(mesh):
    n = mesh.shape["tp"]
    S = n // 2

    def step(x, dy, pre, w_in, w_down):
        R, D = x.shape
        F = pre.shape[1]
        sds = jax.ShapeDtypeStruct
        dma = pltpu.SemaphoreType.DMA
        dx, dw_in, dw_down, *_ = pl.pallas_call(
            functools.partial(kernel, n),
            out_shape=(
                sds((R, D), BF16), sds((D, F), BF16), sds((F, D), BF16),
                sds((2, 2 * S, R, D), BF16), sds((S - 1, SUB, R, D // SUB), BF16), sds((S // 2, SUB, 2, R, D // SUB), BF16),
            ),
            in_specs=[pl.BlockSpec(memory_space=pl.ANY)] * 5,
            out_specs=[pl.BlockSpec(memory_space=pl.ANY)] * 6,
            scratch_shapes=[
                pltpu.VMEM((2, S, R, F), BF16), pltpu.VMEM((D, F), BF16),
                dma((2 * (S - 1), 2, SUB)), dma((2 * (S - 1),)), dma((2 * S,)), dma((2 * S,)),
                dma((S - 1, 2, SUB)), dma((2, 2, SUB)), dma((S // 2, SUB)), dma((2, SUB)),
                dma((2,)), dma((2, 2)), dma((2,)), dma((2,)), dma((2 + SUB,)),
            ],
            compiler_params=pltpu.CompilerParams(collective_id=0, has_side_effects=True, vmem_limit_bytes=63 * 2**20),
            name="mlp_backward",
        )(x, dy, pre, w_in, w_down)
        return dx, dw_in, dw_down

    rows, cols = P(("dp", "tp"), None), P("dp", "tp")
    return jax.shard_map(
        step, mesh=mesh, in_specs=(rows, rows, cols, P(None, "tp"), P("tp", None)),
        out_specs=(rows, cols, rows), check_vma=False,
    )
```

time: 702 us -> 553 us (0.79)
  Pallas kernels: 0 us -> 526 us
  matrix products: 359 us -> 0 us
  waiting for transfers between devices: 289 us -> 0 us
  other arithmetic: 16.6 us -> 0.01 us
  between operations: 13.8 us -> 0.67 us
    pallas_call x0 -> x1, Pallas kernels: none -> 526 us  [step(): pl.pallas_call(functools.partial(kernel, n), out_shape=(sds((R, D), BF16)...]
    dot_general x4 -> x0, matrix products: 359 us -> none  [the longest x2 183 us: by_group(): jnp.einsum('gta,gtb->gab', a, b, preferred_element_type=jnp.float32)]
    unnamed x6 -> x0, waiting for transfers between devices: 289 us -> none
    dot_general x1 -> x0, other arithmetic: 16.6 us -> none  [by_group(): jnp.einsum('gta,gtb->gab', a, b, preferred_element_type=jnp.float32)]
    unnamed x1 -> x11, local copies, waits for them, and re-layouts: 22.4 us -> 25.4 us
  transfers between devices with their start and end apart: 3 -> 0, of which waited for: 3 -> 0; matrix products, arithmetic and copies ran while one was open for 57% -> 0% of each run, Pallas kernels for 0% -> 0%
where the time goes in v1:
time: 553 us; the launch traced here: 552 us
  Pallas kernels  526 us (95%)
  local copies, waits for them, and re-layouts  25.4 us (5%)
    pallas_call x1, Pallas kernels, step(): pl.pallas_call(functools.partial(kernel, n), out_shape=(sds((R, D), BF16)...  526 us
    unnamed x11, local copies, waits for them, and re-layouts  25.4 us

profile of v1, /device:TPU:97, one launch (start us, length us, event | category | flops | bytes accessed | tf_op | source)
XLA Modules:
  0.0 552.1 jit_solution(9534354146627403195)
XLA Ops:
  0.6 526.0 %mlp_backward.1 = (bf16[128,8192]{1,0:T(8,128)(2,1)}, bf16[8192,1024]{1,0:T(8,128)(2,1)}, bf16[1024,8192]{1,0:T(8,128)(2,1)}, bf16[2,32,128,8192]{3,2,1,0:T(8,12...) custom-call(bf16[128,8192]{1,0:T(8,128)(2,1)} %x.1, bf16[128,8192]{1,0:T(8,128)(2,1)} %dy.1, ...), custom_call_target="tpu_custom_call" | custom-call | tf_op jit(solution)/shard_map/mlp_backward/pallas_call | solution.py:360
  526.6 0.0 slice-start
  526.6 3.2 copy.11
  529.9 0.0 slice-start.1
  529.9 0.0 slice-start.2
  529.9 0.0 slice-start.3
  529.9 16.0 %copy.12 = bf16[8192,1024]{1,0:T(8,128)(2,1)} copy(bf16[8192,1024]{1,0:T(8,128)(2,1)} %get-tuple-element.13) | data formatting | bytes 33554432
  545.9 0.0 slice-done
  545.9 0.0 slice-done.1
  545.9 0.0 slice-done.2
  545.9 0.0 slice-done.3
  545.9 6.2 %copy.13 = bf16[1024,8192]{1,0:T(8,128)(2,1)} copy(bf16[1024,8192]{1,0:T(8,128)(2,1)S(1)} %bitcast.1) | data formatting | bytes 33554432
  (1 shorter events, 0.0 us)
Async XLA Ops:
  526.6 19.3 %slice-start = ((s8[16777216]{0:T(1024)(128)(4,1)}), s8[4194304]{0:T(1024)(128)(4,1)S(1)}, s32[]{:S(2)}) async-start(s8[16777216]{0:T(1024)(128)(4,1)} %bitcast), calls=%async_computation | async-start | bytes 8388608
  529.9 16.0 %slice-start.1 = ((s8[16777216]{0:T(1024)(128)(4,1)}), s8[4194304]{0:T(1024)(128)(4,1)S(1)}, s32[]{:S(2)}) async-start(s8[16777216]{0:T(1024)(128)(4,1)} %bitcast), calls=%async_computation.1 | async-start | bytes 8388608
  529.9 16.0 %slice-start.2 = ((s8[16777216]{0:T(1024)(128)(4,1)}), s8[4194304]{0:T(1024)(128)(4,1)S(1)}, s32[]{:S(2)}) async-start(s8[16777216]{0:T(1024)(128)(4,1)} %bitcast), calls=%async_computation.2 | async-start | bytes 8388608
  529.9 16.0 %slice-start.3 = ((s8[16777216]{0:T(1024)(128)(4,1)}), s8[4194304]{0:T(1024)(128)(4,1)S(1)}, s32[]{:S(2)}) async-start(s8[16777216]{0:T(1024)(128)(4,1)} %bitcast), calls=%async_computation.3 | async-start | bytes 8388608

commit v2 on v1

v2 whole, which is shorter than its diff:
```python
import functools
import math

import jax
import jax.numpy as jnp
from jax import lax
from jax.experimental import pallas as pl
from jax.experimental.pallas import tpu as pltpu
from jax.sharding import PartitionSpec as P

MESH = pl.DeviceIdType.MESH
F32, BF16 = jnp.float32, jnp.bfloat16
SUB = 4
TILE = 256
VMEM_LIMIT = 63 * 2**20


def ring_pos(side, chip, ring):
    a, b = chip // side, chip % side
    return jnp.where(ring == 0, a, b) * side + (a + b) % side


def ring_chip(side, pos, ring):
    pos = (pos + side * side) % (side * side)
    major = pos // side
    minor = (pos % side - major + side) % side
    return jnp.where(ring == 0, major * side + minor, minor * side + major)


def ring_perms(n):
    S = n // 2
    side = math.isqrt(S)
    with jax.ensure_compile_time_eval():
        ring = [[int(ring_chip(side, p, c)) * 2 + c for p in range(S)] for c in range(2)]
    return [[(r[p], r[(p + d) % S]) for r in ring for p in range(S)] for d in (1, -1)]


def dot(a, b, ca, cb):
    return lax.dot_general(a, b, (((ca,), (cb,)), ((), ())), preferred_element_type=F32)


def gelu_and_slope(p):
    c = math.sqrt(2.0 / math.pi)
    sq = p * p
    t = jnp.tanh(c * (p + 0.044715 * (sq * p)))
    cdf = 0.5 * (1.0 + t)
    slope = cdf + p * (0.5 * (1.0 - t * t)) * (c * (1.0 + 3 * 0.044715 * sq))
    return p * cdf, slope


def kernel(n, x, dy, pre, w_in, w_down, snd0, snd1, terms, dw_in, dw_down, gb, rsb, sbb, dpre, w2,
           agr, ags, d2r, d2s, rsr, rss, sbr, sbs, wsem, psem, osem, lsem, tsem, fsem):
    S = n // 2
    G = S // 2
    side = math.isqrt(S)
    R, D = x.shape
    H, Q, F = R // 2, R // SUB, pre.shape[1]
    DC, FC = D // SUB, F // SUB
    NT = D // TILE
    me = lax.axis_index("tp")
    chip, core = me // 2, me % 2
    pos, pos2 = ring_pos(side, chip, core), ring_pos(side, chip, 1 - core)
    nxt = [ring_chip(side, pos + 1, core) * 2 + core, ring_chip(side, pos - 1, core) * 2 + core]
    sib = chip * 2 + 1 - core

    def remote(src, dst, ssem, rsem, dev):
        return pltpu.make_async_remote_copy(src, dst, ssem, rsem, device_id={"tp": dev}, device_id_type=MESH)

    def land(v, d):
        return S * (v // G) + jnp.where(v % G == G - 1, S - 2, 2 * (v % G) + d)

    def ag_copy(v, d, q, src=None):
        rows = pl.ds(q * Q if isinstance(q, int) else pl.multiple_of(q * Q, Q), Q)
        slot = S * (v // G) + jnp.where(v % G == 0, S - 1, 2 * (v % G - 1) + d)
        src = gb.at[0, slot, rows] if src is None else src.at[rows]
        return remote(src, gb.at[0, land(v, d), rows], ags.at[v, d], agr.at[v, d, q], nxt[d])

    def goes(v, d, q):
        return (v % G < G - 1) | ((q >= SUB // 2) if d else (q < SUB // 2))

    def d2d_part(w, q):
        rows = pl.ds(pl.multiple_of(q * Q, Q), Q)
        return remote(gb.at[0, w, rows], gb.at[1, w, rows], d2s.at[w], d2r.at[w], sib)

    def d2d(w, src=None):
        return remote(gb.at[0, w] if src is None else src, gb.at[1, w], d2s.at[w], d2r.at[w], sib)

    def pump(v, q):
        for d in range(2):
            @pl.when(goes(v, d, q))
            def _():
                ag_copy(v, d, q).wait_recv()

                @pl.when((v % G < G - 1) & goes(v + 1, d, q))
                def _():
                    ag_copy(v + 1, d, q).start()

                d2d_part(land(v, d), q).start()

        @pl.when((v == G - 2) & (q == SUB - 1))
        def _():
            for p in range(SUB):
                for d in range(2):
                    ag_copy(G, d, p).start()

    bar = pltpu.get_barrier_semaphore()
    for dev in (*nxt, sib):
        pl.semaphore_signal(bar, inc=1, device_id={"tp": dev}, device_id_type=MESH)
    pl.semaphore_wait(bar, 3)
    for q in range(SUB):
        for d in range(2):
            ag_copy(0, d, q, dy).start()
    d2d(S - 1, dy).start()
    d2d(2 * S - 1, x).start()

    def first(hT):
        def p1(w1, a, prb, wst):
            load_w1 = pltpu.make_async_copy(w_down, w1, wsem.at[0])
            own = [pltpu.make_async_copy(src, a.at[0, i], lsem.at[i]) for i, src in enumerate((dy, x))]
            put = [pltpu.make_async_copy(a.at[0, i], gb.at[0, (i + 1) * S - 1], lsem.at[i]) for i in range(2)]
            for c in own:
                c.start()
            load_w1.start()
            for o, c in zip(own, put):
                o.wait()
                c.start()
            for c in put:
                c.wait()

            def slot_of(u):
                return (u + S - 1) % S

            def loads(u):
                e, b = slot_of(u), u % 2
                out = [pltpu.make_async_copy(gb.at[:, e], a.at[b], lsem.at[b])]
                away = jnp.where(e == S - 1, 0, jnp.where(e == S - 2, S // 2, jnp.where(e % 2 == 0, S - 1 - e // 2, e // 2 + 1)))
                for h, (ps, cr) in enumerate(((pos, core), (pos2, 1 - core))):
                    row = pl.multiple_of((ring_chip(side, ps + away - S, cr) * 2 + cr) * R, R)
                    out.append(pltpu.make_async_copy(pre.at[pl.ds(row, R)], prb.at[b, h], psem.at[b, h]))
                rows = pl.ds(pl.multiple_of(u * (D // S), D // S), D // S)
                out.append(pltpu.make_async_copy(w_in.at[rows], wst, wsem.at[1]))
                return out

            def fetch(u):
                d2d(slot_of(u)).wait_recv()
                for c in loads(u):
                    c.start()

            fetch(0)
            load_w1.wait()

            @pl.loop(0, G + 1)
            def _(v):
                @pl.loop(0, 2)
                def _(half):
                    u = 2 * v - 1 + half
                    busy = (u >= 0) & (u < S) & ((v > 0) | (half == 1))

                    @pl.loop(0, SUB)
                    def _(j):
                        @pl.when(j % 2 == 0)
                        def _():
                            pump(v, half * (SUB // 2) + j // 2)

                        @pl.when(busy)
                        def _():
                            b = u % 2

                            @pl.when(j == 0)
                            def _():
                                for c in loads(u):
                                    c.wait()

                                w2[:, pl.ds(pl.multiple_of(u * (D // S), D // S), D // S)] = wst[...].T

                                @pl.when((half == 0) & (u + 1 < S))
                                def _():
                                    fetch(u + 1)

                            cols = pl.ds(pl.multiple_of(j * FC, FC), FC)
                            dh = dot(a[b].reshape(2 * R, D), w1[cols, :], 1, 1)
                            for h in range(2):
                                hid, slope = gelu_and_slope(prb[b, h, :, cols].astype(F32))
                                dpre[h, slot_of(u), :, cols] = (dh[h * R : (h + 1) * R] * slope).astype(BF16)
                                tok = pl.ds(pl.multiple_of((h * S + slot_of(u)) * R, R), R)
                                hT[cols, tok] = hid.T.astype(BF16)

                            @pl.when((j == SUB - 1) & (half == 1) & (u + 1 < S))
                            def _():
                                fetch(u + 1)

        pl.run_scoped(p1, pltpu.VMEM((F, D), BF16), pltpu.VMEM((2, 2, R, D), BF16), pltpu.VMEM((2, 2, R, F), BF16),
                      pltpu.VMEM((D // S, F), BF16))

        def p2(tile, dout, sst):
            def tile_load(i):
                cols = pl.ds(pl.multiple_of(i * TILE, TILE), TILE)
                return pltpu.make_async_copy(gb.at[:, pl.ds(0, S), :, cols], tile.at[i % 2], tsem.at[i % 2])

            def tile_out(i):
                cols = pl.ds(pl.multiple_of(i * TILE, TILE), TILE)
                return pltpu.make_async_copy(dout.at[i % 2], dw_down.at[:, cols], osem.at[i % 2])

            def sib_copy(k, c):
                return remote(sst.at[k % 2, c], sbb.at[k, c], sbs.at[k % 2, c], sbr.at[k, c], sib)

            tile_load(0).start()

            @pl.loop(0, S)
            def _(g):
                def step(w):
                    @pl.when(w % 2 == 0)
                    def _():
                        pump(G + 1 + w // (2 * SUB), (w // 2) % SUB)

                @pl.loop(0, 2)
                def _(j):
                    step(3 * g + j)
                    i = 2 * g + j
                    tile_load(i).wait()

                    @pl.when(i + 1 < NT)
                    def _():
                        tile_load(i + 1).start()

                    @pl.when(i >= 2)
                    def _():
                        tile_out(i - 2).wait()

                    dout[i % 2] = dot(hT[...], tile[i % 2].reshape(2 * S * R, TILE), 1, 0).astype(BF16)
                    tile_out(i).start()

                step(3 * g + 2)

                @pl.loop(0, 2)
                def _(j):
                    k, c = G - 1 - g // 2, (g % 2) * 2 + j

                    @pl.when(g >= 4)
                    def _():
                        sib_copy(k + 2, c).wait_send()

                    part = dot(dpre[1, pl.ds(2 * k, 2)].reshape(2 * R, F), w2[:, pl.ds(pl.multiple_of(c * DC, DC), DC)], 1, 0)
                    sst[k % 2, c] = part.astype(BF16).reshape(2, R, DC)
                    sib_copy(k, c).start()

            for i in range(NT - 2, NT):
                tile_out(i).wait()

            for k in range(2):
                for c in range(SUB):
                    sib_copy(k, c).wait_send()

        pl.run_scoped(p2, pltpu.VMEM((2, 2, S, R, TILE), BF16), pltpu.VMEM((2, F, TILE), BF16), pltpu.VMEM((2, SUB, 2, R, DC), BF16))

    pl.run_scoped(first, pltpu.VMEM((F, 2 * S * R), BF16))

    def p3(own, xt, eo, got, gsib, out, tb):
        def x_load(i):
            cols = pl.ds(pl.multiple_of(i * TILE, TILE), TILE)
            return pltpu.make_async_copy(gb.at[:, pl.ds(S, S), :, cols], xt.at[i % 2], tsem.at[i % 2])

        def e_out(i):
            return pltpu.make_async_copy(eo.at[i % 2], dw_in.at[pl.ds(pl.multiple_of(i * TILE, TILE), TILE)], osem.at[i % 2])

        def rs_copy(r, i, q):
            return remote(out.at[r % 2, q, i], rsb.at[r, q, i], rss.at[r % 2, i, q], rsr.at[r, i, q], nxt[1 - i])

        def rs_half(i, q):
            rows = pl.ds(H * (1 - i), H)
            return remote(out.at[0, q, 0, rows], rsb.at[0, q, i, rows], rss.at[0, i, q], rsr.at[0, i, q], nxt[1 - i])

        def got_load(r, q):
            return pltpu.make_async_copy(rsb.at[r - 1, q], got.at[q % 2], lsem.at[q % 2])

        def got_half(i, q):
            rows = pl.ds(H * (1 - i), H)
            return pltpu.make_async_copy(rsb.at[0, q, i, rows], got.at[q % 2, i, rows], fsem.at[2 + i, q])

        def sib_load(r, q):
            return pltpu.make_async_copy(sbb.at[G - 1 - r, q], gsib.at[q % 2], psem.at[0, q % 2])

        def sib_arrive(r, q):
            remote(sbb.at[G - 1 - r, q], sbb.at[G - 1 - r, q], sbs.at[0, q], sbr.at[G - 1 - r, q], sib).wait_recv()

        def col(q):
            return pl.ds(pl.multiple_of(q * DC, DC), DC)

        def snd_out(q):
            return [pltpu.make_async_copy(out.at[(G - 1) % 2, q, i], snd.at[:, col(q)], fsem.at[i, q]) for i, snd in ((1, snd0), (0, snd1))]

        def term_out(q):
            return pltpu.make_async_copy(tb.at[q % 2], terms.at[:, col(q)], wsem.at[1 + q % 2])

        got[...] = jnp.zeros_like(got)
        sib_arrive(0, 0)
        sib_load(0, 0).start()

        @pl.loop(0, G)
        def _(r):
            @pl.loop(0, SUB)
            def _(q):
                k = G - 1 - r
                part = dot(dpre[0, pl.ds(2 * k, 2)].reshape(2 * R, F), w2[:, col(q)], 1, 0)
                own[...] = part.reshape(2, R, DC)
                sib_load(r, q).wait()

                @pl.when(r == 0)
                def _():
                    out[0, q, 0] = (own[0] + gsib[q % 2, 0].astype(F32)).astype(BF16)
                    for i in range(2):
                        rs_half(i, q).start()

                    @pl.when(q >= 2)
                    def _():
                        term_out(q - 2).wait()

                    tb[q % 2] = own[1] + gsib[q % 2, 1].astype(F32)
                    term_out(q).start()
                    pump(2 * G - 1, q)

                @pl.when(r == 2)
                def _():
                    for i in range(2):
                        rs_half(i, q).wait_send()

                @pl.when(r > 2)
                def _():
                    for i in range(2):
                        rs_copy(r - 2, i, q).wait_send()

                @pl.when(r == 1)
                def _():
                    for i in range(2):
                        got_half(i, q).wait()

                @pl.when(r > 1)
                def _():
                    got_load(r, q).wait()

                @pl.when(r > 0)
                def _():
                    out[r % 2, q] = (own[...] + gsib[q % 2].astype(F32) + got[q % 2].astype(F32)).astype(BF16)

                @pl.when((r > 0) & (r < G - 1))
                def _():
                    for i in range(2):
                        rs_copy(r, i, q).start()

                @pl.when(r == G - 1)
                def _():
                    for c in snd_out(q):
                        c.start()

                @pl.when((r < G - 1) | (q < SUB - 1))
                def _():
                    q1 = (q + 1) % SUB
                    r1 = r + (q + 1) // SUB
                    sib_arrive(r1, q1)
                    sib_load(r1, q1).start()

                    @pl.when(r1 == 1)
                    def _():
                        for i in range(2):
                            rs_half(i, q1).wait_recv()
                            got_half(i, q1).start()

                    @pl.when(r1 > 1)
                    def _():
                        for i in range(2):
                            rs_copy(r1 - 1, i, q1).wait_recv()
                        got_load(r1, q1).start()

                extra = jnp.where(r < G - 2, 1, 0)
                base = SUB * (r - 1) + jnp.minimum(r - 1, G - 3) + q + jnp.where(q > 0, extra, 0)
                count = jnp.where(q == 0, 1 + extra, 1)

                @pl.loop(0, jnp.where(r == 0, 0, jnp.minimum(count, NT - base)))
                def _(jj):
                    i = base + jj

                    @pl.when(i == 0)
                    def _():
                        @pl.loop(S, 2 * S)
                        def _(w):
                            d2d(w).wait_recv()

                        x_load(0).start()

                    x_load(i).wait()

                    @pl.when(i + 1 < NT)
                    def _():
                        x_load(i + 1).start()

                    @pl.when(i >= 2)
                    def _():
                        e_out(i - 2).wait()

                    eo[i % 2] = dot(xt[i % 2].reshape(2 * S * R, TILE), dpre[...].reshape(2 * S * R, F), 0, 0).astype(BF16)
                    e_out(i).start()

        for i in range(NT - 2, NT):
            e_out(i).wait()
        for q in range(SUB):
            for i in range(2):
                rs_copy(G - 2, i, q).wait_send()
            for c in snd_out(q):
                c.wait()
        for q in range(SUB - 2, SUB):
            term_out(q).wait()

    pl.run_scoped(p3, pltpu.VMEM((2, R, DC), F32), pltpu.VMEM((2, 2, S, R, TILE), BF16), pltpu.VMEM((2, TILE, F), BF16),
                  pltpu.VMEM((2, 2, R, DC), BF16), pltpu.VMEM((2, 2, R, DC), BF16), pltpu.VMEM((2, SUB, 2, R, DC), BF16),
                  pltpu.VMEM((2, R, DC), F32))

    @pl.loop(0, 2 * G)
    def _(v):
        for d in range(2):
            @pl.when(v % G < G - 1)
            def _():
                remote(gb.at[0, 0], gb.at[0, 0], ags.at[v, d], agr.at[v, d, 0], nxt[d]).wait_send()

            @pl.when(v % G == G - 1)
            def _():
                half = gb.at[0, 0, pl.ds(0, H)]
                remote(half, half, ags.at[v, d], agr.at[v, d, 0], nxt[d]).wait_send()

    @pl.loop(0, 2 * S)
    def _(w):
        d2d(w).wait_send()


def copy_kernel(src, dst, buf, isem, osem):
    parts = isem.shape[0]
    rows = src.shape[0] // parts
    get = [pltpu.make_async_copy(src.at[pl.ds(i * rows, rows)], buf.at[i], isem.at[i]) for i in range(parts)]
    put = [pltpu.make_async_copy(buf.at[i], dst.at[pl.ds(i * rows, rows)], osem.at[i]) for i in range(parts)]
    for c in get:
        c.start()
    for g, p in zip(get, put):
        g.wait()
        p.start()
    for c in put:
        c.wait()


def copied(a):
    parts = 16
    return pl.pallas_call(
        copy_kernel,
        out_shape=jax.ShapeDtypeStruct(a.shape, a.dtype),
        in_specs=[pl.BlockSpec(memory_space=pl.ANY)],
        out_specs=pl.BlockSpec(memory_space=pl.ANY),
        scratch_shapes=[pltpu.VMEM((parts, a.shape[0] // parts, a.shape[1]), a.dtype), pltpu.SemaphoreType.DMA((parts,)), pltpu.SemaphoreType.DMA((parts,))],
        compiler_params=pltpu.CompilerParams(vmem_limit_bytes=60 * 2**20),
        cost_estimate=pl.CostEstimate(flops=4 * 10**9, bytes_accessed=4 * a.size, transcendentals=0),
        name="copy_out",
    )(a)


def solution(mesh):
    n = mesh.shape["tp"]
    S = n // 2
    G = S // 2
    perms = ring_perms(n)

    def step(x, dy, pre, w_in, w_down):
        R, D = x.shape
        F = pre.shape[1]
        sds = jax.ShapeDtypeStruct
        dma = pltpu.SemaphoreType.DMA
        *sums, term, dw_in, dw_down, _, _, _ = pl.pallas_call(
            functools.partial(kernel, n),
            out_shape=(
                sds((R, D), BF16), sds((R, D), BF16), sds((R, D), F32), sds((D, F), BF16), sds((F, D), BF16),
                sds((2, 2 * S, R, D), BF16), sds((G - 1, SUB, 2, R, D // SUB), BF16), sds((G, SUB, 2, R, D // SUB), BF16),
            ),
            in_specs=[pl.BlockSpec(memory_space=pl.ANY)] * 5,
            out_specs=[pl.BlockSpec(memory_space=pl.ANY)] * 8,
            scratch_shapes=[
                pltpu.VMEM((2, S, R, F), BF16), pltpu.VMEM((F, D), BF16),
                dma((2 * G, 2, SUB)), dma((2 * G, 2)), dma((2 * S,)), dma((2 * S,)),
                dma((G - 1, 2, SUB)), dma((2, 2, SUB)), dma((G, SUB)), dma((2, SUB)),
                dma((3,)), dma((2, 2)), dma((2,)), dma((2,)), dma((2,)), dma((4, SUB)),
            ],
            compiler_params=pltpu.CompilerParams(collective_id=0, has_side_effects=True, vmem_limit_bytes=VMEM_LIMIT),
            name="mlp_backward",
        )(x, dy, pre, w_in, w_down)
        dw_in, dw_down = copied(dw_in), copied(dw_down)
        ahead, back = (lax.ppermute(a, "tp", perm) for a, perm in zip(sums, perms))
        dx = (term + ahead.astype(F32) + back.astype(F32)).astype(BF16)
        return dx, dw_in, dw_down

    rows, cols = P(("dp", "tp"), None), P("dp", "tp")
    return jax.shard_map(
        step, mesh=mesh, in_specs=(rows, rows, cols, P(None, "tp"), P("tp", None)),
        out_specs=(rows, cols, rows), check_vma=False,
    )
```

time: 553 us -> 535 us (0.967)
  local copies, waits for them, and re-layouts: 25.4 us -> 0 us
    unnamed x11 -> x0, local copies, waits for them, and re-layouts: 25.4 us -> none
    pallas_call x1, Pallas kernels: 526 us -> 501 us  [step(): pl.pallas_call(functools.partial(kernel, n), out_shape=(sds((R, D), BF16)...]
    pallas_call x0 -> x2, Pallas kernels: none -> 24 us  [copied(): pl.pallas_call(copy_kernel, out_shape=jax.ShapeDtypeStruct(a.shape, a.dty...]
  transfers between devices with their start and end apart: 0 -> 2, of which waited for: 0 -> 0; matrix products, arithmetic and copies ran while one was open for 0% -> 0% of each run, Pallas kernels for 0% -> 4%
where the time goes in v2:
time: 535 us; the launch traced here: 534 us
  Pallas kernels  525 us (98%)
    pallas_call x1, Pallas kernels, step(): pl.pallas_call(functools.partial(kernel, n), out_shape=(sds((R, D), BF16)...  501 us
    pallas_call x2, Pallas kernels, copied(): pl.pallas_call(copy_kernel, out_shape=jax.ShapeDtypeStruct(a.shape, a.dty...  24 us
  transfers between devices with their start and end apart: 2, of which 0 were waited for; matrix products, arithmetic and copies ran while one was open for 0% of the time, Pallas kernels for 4%

profile of v2, /device:TPU:97, one launch (start us, length us, event | category | flops | bytes accessed | tf_op | source)
XLA Modules:
  0.0 533.6 jit_solution(11415315576256672070)
XLA Ops:
  0.6 501.3 %mlp_backward.1 = (bf16[128,8192]{1,0:T(8,128)(2,1)}, bf16[128,8192]{1,0:T(8,128)(2,1)}, f32[128,8192]{1,0:T(8,128)}, bf16[8192,1024]{1,0:T(8,128)(2,1)}, bf16[1...) custom-call(bf16[128,8192]{1,0:T(8,128)(2,1)} %x.1, ...), custom_call_target="tpu_custom_call" | custom-call | tf_op jit(solution)/shard_map/mlp_backward/pallas_call | solution.py:473
  501.9 0.6 collective-permute-start
  502.5 2.2 collective-permute-start.1
  504.7 12.0 %copy_out.2 = bf16[8192,1024]{1,0:T(8,128)(2,1)} custom-call(bf16[8192,1024]{1,0:T(8,128)(2,1)} %get-tuple-element.11.src), custom_call_target="tpu_custom_call" | custom-call | flops 4000000000 | bytes 33554432 | tf_op jit(solution)/shard_map/copy_out/pallas_call | solution.py:450
  516.7 12.0 %copy_out.3 = bf16[1024,8192]{1,0:T(8,128)(2,1)} custom-call(bf16[1024,8192]{1,0:T(8,128)(2,1)} %get-tuple-element.12.src), custom_call_target="tpu_custom_call" | custom-call | flops 4000000000 | bytes 33554432 | tf_op jit(solution)/shard_map/copy_out/pallas_call | solution.py:450
  528.7 0.0 collective-permute-done
  528.7 0.0 collective-permute-done.1
  528.7 4.9 add_convert_fusion
Async XLA Ops:
  501.9 26.7 %collective-permute-start = (bf16[128,8192]{1,0:T(8,128)(2,1)}, bf16[128,8192]{1,0:T(8,128)(2,1)S(1)}, u32[]{:S(2)}, u32[]{:S(2)}) collective-permute-start(bf16[128,8192]{1,0:T(8,128)(2,1)} %get-tuple-element.9), channel_id=1, source_target_pairs={{0,2},{2,4},{4,6},{6,14},{14,8},{8,10},{10,12},{12,20},{20,22},{22... | collective-permute-start | bytes 6291464 | tf_op jit(solution)/shard_map/ppermute | solution.py:491
  502.5 26.1 %collective-permute-start.1 = (bf16[128,8192]{1,0:T(8,128)(2,1)}, bf16[128,8192]{1,0:T(8,128)(2,1)}, u32[]{:S(2)}, u32[]{:S(2)}) collective-permute-start(bf16[128,8192]{1,0:T(8,128)(2,1)} %get-tuple-element.10), channel_id=1, source_target_pairs={{0,24},{2,0},{4,2},{6,4},{14,6},{8,14},{10,8},{12,10},{20,12},{22,... | collective-permute-start | bytes 6291464 | tf_op jit(solution)/shard_map/ppermute | solution.py:491

commit v3 on v2

--- a/solution.py
+++ b/solution.py
@@ -213,24 +213,7 @@
                     def _():
                         pump(G + 1 + w // (2 * SUB), (w // 2) % SUB)
 
-                @pl.loop(0, 2)
-                def _(j):
-                    step(3 * g + j)
-                    i = 2 * g + j
-                    tile_load(i).wait()
-
-                    @pl.when(i + 1 < NT)
-                    def _():
-                        tile_load(i + 1).start()
-
-                    @pl.when(i >= 2)
-                    def _():
-                        tile_out(i - 2).wait()
-
-                    dout[i % 2] = dot(hT[...], tile[i % 2].reshape(2 * S * R, TILE), 1, 0).astype(BF16)
-                    tile_out(i).start()
-
-                step(3 * g + 2)
+                step(3 * g)
 
                 @pl.loop(0, 2)
                 def _(j):
@@ -244,6 +227,23 @@
                     sst[k % 2, c] = part.astype(BF16).reshape(2, R, DC)
                     sib_copy(k, c).start()
 
+                @pl.loop(0, 2)
+                def _(j):
+                    step(3 * g + 1 + j)
+                    i = 2 * g + j
+                    tile_load(i).wait()
+
+                    @pl.when(i + 1 < NT)
+                    def _():
+                        tile_load(i + 1).start()
+
+                    @pl.when(i >= 2)
+                    def _():
+                        tile_out(i - 2).wait()
+
+                    dout[i % 2] = dot(hT[...], tile[i % 2].reshape(2 * S * R, TILE), 1, 0).astype(BF16)
+                    tile_out(i).start()
+
             for i in range(NT - 2, NT):
                 tile_out(i).wait()
 
@@ -254,6 +254,23 @@
         pl.run_scoped(p2, pltpu.VMEM((2, 2, S, R, TILE), BF16), pltpu.VMEM((2, F, TILE), BF16), pltpu.VMEM((2, SUB, 2, R, DC), BF16))
 
     pl.run_scoped(first, pltpu.VMEM((F, 2 * S * R), BF16))
+
+    def sent():
+        @pl.loop(0, 2 * G)
+        def _(v):
+            for d in range(2):
+                @pl.when(v % G < G - 1)
+                def _():
+                    remote(gb.at[0, 0], gb.at[0, 0], ags.at[v, d], agr.at[v, d, 0], nxt[d]).wait_send()
+
+                @pl.when(v % G == G - 1)
+                def _():
+                    half = gb.at[0, 0, pl.ds(0, H)]
+                    remote(half, half, ags.at[v, d], agr.at[v, d, 0], nxt[d]).wait_send()
+
+        @pl.loop(0, 2 * S)
+        def _(w):
+            d2d(w).wait_send()
 
     def p3(own, xt, eo, got, gsib, out, tb):
         def x_load(i):
@@ -270,8 +287,8 @@
             rows = pl.ds(H * (1 - i), H)
             return remote(out.at[0, q, 0, rows], rsb.at[0, q, i, rows], rss.at[0, i, q], rsr.at[0, i, q], nxt[1 - i])
 
-        def got_load(r, q):
-            return pltpu.make_async_copy(rsb.at[r - 1, q], got.at[q % 2], lsem.at[q % 2])
+        def got_load(r, i, q):
+            return pltpu.make_async_copy(rsb.at[r - 1, q, i], got.at[q % 2, i], fsem.at[2 + i, q])
 
         def got_half(i, q):
             rows = pl.ds(H * (1 - i), H)
@@ -286,23 +303,29 @@
         def col(q):
             return pl.ds(pl.multiple_of(q * DC, DC), DC)
 
-        def snd_out(q):
-            return [pltpu.make_async_copy(out.at[(G - 1) % 2, q, i], snd.at[:, col(q)], fsem.at[i, q]) for i, snd in ((1, snd0), (0, snd1))]
+        def snd_out(i, q):
+            return pltpu.make_async_copy(out.at[(G - 1) % 2, q, i], (snd1, snd0)[i].at[:, col(q)], fsem.at[i, q])
 
         def term_out(q):
             return pltpu.make_async_copy(tb.at[q % 2], terms.at[:, col(q)], wsem.at[1 + q % 2])
 
-        got[...] = jnp.zeros_like(got)
+        def own_terms(r, q):
+            k = G - 1 - r
+            part = dot(dpre[0, pl.ds(2 * k, 2)].reshape(2 * R, F), w2[:, col(q)], 1, 0)
+            own[...] = part.reshape(2, R, DC)
+
         sib_arrive(0, 0)
         sib_load(0, 0).start()
+        own_terms(0, 0)
 
         @pl.loop(0, G)
         def _(r):
             @pl.loop(0, SUB)
             def _(q):
-                k = G - 1 - r
-                part = dot(dpre[0, pl.ds(2 * k, 2)].reshape(2 * R, F), w2[:, col(q)], 1, 0)
-                own[...] = part.reshape(2, R, DC)
+                @pl.when((r == 0) & (q == 0))
+                def _():
+                    got[...] = jnp.zeros_like(got)
+
                 sib_load(r, q).wait()
 
                 @pl.when(r == 0)
@@ -324,33 +347,30 @@
                     for i in range(2):
                         rs_half(i, q).wait_send()
 
-                @pl.when(r > 2)
-                def _():
-                    for i in range(2):
+                for i in range(2):
+                    @pl.when(r > 2)
+                    def _():
                         rs_copy(r - 2, i, q).wait_send()
 
-                @pl.when(r == 1)
-                def _():
-                    for i in range(2):
+                    @pl.when(r == 1)
+                    def _():
                         got_half(i, q).wait()
 
-                @pl.when(r > 1)
-                def _():
-                    got_load(r, q).wait()
-
-                @pl.when(r > 0)
-                def _():
-                    out[r % 2, q] = (own[...] + gsib[q % 2].astype(F32) + got[q % 2].astype(F32)).astype(BF16)
-
-                @pl.when((r > 0) & (r < G - 1))
-                def _():
-                    for i in range(2):
+                    @pl.when(r > 1)
+                    def _():
+                        got_load(r, i, q).wait()
+
+                    @pl.when(r > 0)
+                    def _():
+                        out[r % 2, q, i] = (own[i] + gsib[q % 2, i].astype(F32) + got[q % 2, i].astype(F32)).astype(BF16)
+
+                    @pl.when((r > 0) & (r < G - 1))
+                    def _():
                         rs_copy(r, i, q).start()
 
-                @pl.when(r == G - 1)
-                def _():
-                    for c in snd_out(q):
-                        c.start()
+                    @pl.when(r == G - 1)
+                    def _():
+                        snd_out(i, q).start()
 
                 @pl.when((r < G - 1) | (q < SUB - 1))
                 def _():
@@ -358,6 +378,7 @@
                     r1 = r + (q + 1) // SUB
                     sib_arrive(r1, q1)
                     sib_load(r1, q1).start()
+                    own_terms(r1, q1)
 
                     @pl.when(r1 == 1)
                     def _():
@@ -369,10 +390,10 @@
                     def _():
                         for i in range(2):
                             rs_copy(r1 - 1, i, q1).wait_recv()
-                        got_load(r1, q1).start()
-
-                extra = jnp.where(r < G - 2, 1, 0)
-                base = SUB * (r - 1) + jnp.minimum(r - 1, G - 3) + q + jnp.where(q > 0, extra, 0)
+                            got_load(r1, i, q1).start()
+
+                extra = jnp.where(r < G - 1, 1, 0)
+                base = (SUB + 1) * (r - 1) + q + jnp.where(q > 0, extra, 0)
                 count = jnp.where(q == 0, 1 + extra, 1)
 
                 @pl.loop(0, jnp.where(r == 0, 0, jnp.minimum(count, NT - base)))
@@ -388,6 +409,10 @@
                         x_load(0).start()
 
                     x_load(i).wait()
+
+                    @pl.when(i == NT // 2)
+                    def _():
+                        sent()
 
                     @pl.when(i + 1 < NT)
                     def _():
@@ -405,8 +430,8 @@
         for q in range(SUB):
             for i in range(2):
                 rs_copy(G - 2, i, q).wait_send()
-            for c in snd_out(q):
-                c.wait()
+            for i in range(2):
+                snd_out(i, q).wait()
         for q in range(SUB - 2, SUB):
             term_out(q).wait()
 
@@ -414,28 +439,15 @@
                   pltpu.VMEM((2, 2, R, DC), BF16), pltpu.VMEM((2, 2, R, DC), BF16), pltpu.VMEM((2, SUB, 2, R, DC), BF16),
                   pltpu.VMEM((2, R, DC), F32))
 
-    @pl.loop(0, 2 * G)
-    def _(v):
-        for d in range(2):
-            @pl.when(v % G < G - 1)
-            def _():
-                remote(gb.at[0, 0], gb.at[0, 0], ags.at[v, d], agr.at[v, d, 0], nxt[d]).wait_send()
-
-            @pl.when(v % G == G - 1)
-            def _():
-                half = gb.at[0, 0, pl.ds(0, H)]
-                remote(half, half, ags.at[v, d], agr.at[v, d, 0], nxt[d]).wait_send()
-
-    @pl.loop(0, 2 * S)
-    def _(w):
-        d2d(w).wait_send()
-
-
-def copy_kernel(src, dst, buf, isem, osem):
-    parts = isem.shape[0]
-    rows = src.shape[0] // parts
-    get = [pltpu.make_async_copy(src.at[pl.ds(i * rows, rows)], buf.at[i], isem.at[i]) for i in range(parts)]
-    put = [pltpu.make_async_copy(buf.at[i], dst.at[pl.ds(i * rows, rows)], osem.at[i]) for i in range(parts)]
+
+def copy_kernel(a, b, a2, b2, abuf, bbuf, isem, osem):
+    get, put = [], []
+    for src, dst, buf in ((a, a2, abuf), (b, b2, bbuf)):
+        parts, rows = buf.shape[:2]
+        for i in range(parts):
+            at = pl.ds(i * rows, rows)
+            get.append(pltpu.make_async_copy(src.at[at], buf.at[i], isem.at[len(get)]))
+            put.append(pltpu.make_async_copy(buf.at[i], dst.at[at], osem.at[len(put)]))
     for c in get:
         c.start()
     for g, p in zip(get, put):
@@ -445,18 +457,31 @@
         c.wait()
 
 
-def copied(a):
-    parts = 16
+def copied(a, b):
+    parts = 4
+    dma = pltpu.SemaphoreType.DMA
     return pl.pallas_call(
         copy_kernel,
-        out_shape=jax.ShapeDtypeStruct(a.shape, a.dtype),
-        in_specs=[pl.BlockSpec(memory_space=pl.ANY)],
-        out_specs=pl.BlockSpec(memory_space=pl.ANY),
-        scratch_shapes=[pltpu.VMEM((parts, a.shape[0] // parts, a.shape[1]), a.dtype), pltpu.SemaphoreType.DMA((parts,)), pltpu.SemaphoreType.DMA((parts,))],
-        compiler_params=pltpu.CompilerParams(vmem_limit_bytes=60 * 2**20),
-        cost_estimate=pl.CostEstimate(flops=4 * 10**9, bytes_accessed=4 * a.size, transcendentals=0),
+        out_shape=[jax.ShapeDtypeStruct(t.shape, t.dtype) for t in (a, b)],
+        in_specs=[pl.BlockSpec(memory_space=pl.ANY)] * 2,
+        out_specs=[pl.BlockSpec(memory_space=pl.ANY)] * 2,
+        scratch_shapes=[pltpu.VMEM((parts, t.shape[0] // parts, t.shape[1]), t.dtype) for t in (a, b)] + [dma((2 * parts,))] * 2,
+        compiler_params=pltpu.CompilerParams(vmem_limit_bytes=48 * 2**20),
+        cost_estimate=pl.CostEstimate(flops=8 * 10**9, bytes_accessed=8 * a.size, transcendentals=0),
         name="copy_out",
-    )(a)
+    )(a, b)
+
+
+def add_kernel(a, b, c, o):
+    o[...] = (a[...] + b[...].astype(F32) + c[...].astype(F32)).astype(BF16)
+
+
+def added(term, ahead, back):
+    whole = pl.BlockSpec(memory_space=pltpu.VMEM)
+    return pl.pallas_call(
+        add_kernel, in_specs=[whole] * 3, out_specs=whole, out_shape=jax.ShapeDtypeStruct(term.shape, BF16), name="last_add",
+        compiler_params=pltpu.CompilerParams(vmem_limit_bytes=16 * 2**20),
+    )(term, ahead, back)
 
 
 def solution(mesh):
@@ -487,10 +512,9 @@
             compiler_params=pltpu.CompilerParams(collective_id=0, has_side_effects=True, vmem_limit_bytes=VMEM_LIMIT),
             name="mlp_backward",
         )(x, dy, pre, w_in, w_down)
-        dw_in, dw_down = copied(dw_in), copied(dw_down)
+        dw_in, dw_down = copied(dw_in, dw_down)
         ahead, back = (lax.ppermute(a, "tp", perm) for a, perm in zip(sums, perms))
-        dx = (term + ahead.astype(F32) + back.astype(F32)).astype(BF16)
-        return dx, dw_in, dw_down
+        return added(term, ahead, back), dw_in, dw_down
 
     rows, cols = P(("dp", "tp"), None), P("dp", "tp")
     return jax.shard_map(

time: 535 us -> 528 us (0.987)
  transfers between devices with their start and end apart: 2 -> 2, of which waited for: 0 -> 1; matrix products, arithmetic and copies ran while one was open for 0% -> 0% of each run, Pallas kernels for 4% -> 4%
where the time goes in v3:
time: 528 us; the launch traced here: 527 us
  Pallas kernels  522 us (99%)
    pallas_call x1, Pallas kernels, step(): pl.pallas_call(functools.partial(kernel, n), out_shape=(sds((R, D), BF16)...  498 us
    pallas_call x1, Pallas kernels, copied(): pl.pallas_call(copy_kernel, out_shape=[jax.ShapeDtypeStruct(t.shape, t.dt...  22.6 us
  transfers between devices with their start and end apart: 2, of which 1 were waited for; matrix products, arithmetic and copies ran while one was open for 0% of the time, Pallas kernels for 4%

profile of v3, /device:TPU:97, one launch (start us, length us, event | category | flops | bytes accessed | tf_op | source)
XLA Modules:
  0.0 527.0 jit_solution(10273355877060110955)
XLA Ops:
  0.6 497.9 %mlp_backward.1 = (bf16[128,8192]{1,0:T(8,128)(2,1)}, bf16[128,8192]{1,0:T(8,128)(2,1)}, f32[128,8192]{1,0:T(8,128)}, bf16[8192,1024]{1,0:T(8,128)(2,1)}, bf16[1...) custom-call(bf16[128,8192]{1,0:T(8,128)(2,1)} %x.1, ...), custom_call_target="tpu_custom_call" | custom-call | tf_op jit(solution)/shard_map/mlp_backward/pallas_call | solution.py:498
  498.6 0.5 collective-permute-start
  499.0 2.3 collective-permute-start.1
  501.4 0.0 copy-start
  501.4 22.6 %copy_out.1 = (bf16[8192,1024]{1,0:T(8,128)(2,1)}, bf16[1024,8192]{1,0:T(8,128)(2,1)}) custom-call(bf16[8192,1024]{1,0:T(8,128)(2,1)} %get-tuple-element.13.a, bf16[1024,8192]{1,0:T(8,128)(2,1)} %get-tuple-element.14.b), custom_call_target="tpu_custom_call" | custom-call | flops 8000000000 | bytes 67108864 | tf_op jit(solution)/shard_map/copy_out/pallas_call | solution.py:463
  523.9 1.1 collective-permute-done.b
  525.1 0.0 collective-permute-done.1.c
  525.1 0.0 copy-done
  525.1 1.9 last_add.1
Async XLA Ops:
  498.6 26.5 %collective-permute-start = (bf16[128,8192]{1,0:T(8,128)(2,1)}, bf16[128,8192]{1,0:T(8,128)(2,1)S(1)}, u32[]{:S(2)}, u32[]{:S(2)}) collective-permute-start(bf16[128,8192]{1,0:T(8,128)(2,1)} %get-tuple-element.11), channel_id=1, source_target_pairs={{0,2},{2,4},{4,6},{6,14},{14,8},{8,10},{10,12},{12,20},{20,22},{22... | collective-permute-start | bytes 6291464 | tf_op jit(solution)/shard_map/ppermute | solution.py:516
  499.0 26.0 %collective-permute-start.1 = (bf16[128,8192]{1,0:T(8,128)(2,1)}, bf16[128,8192]{1,0:T(8,128)(2,1)S(1)}, u32[]{:S(2)}, u32[]{:S(2)}) collective-permute-start(bf16[128,8192]{1,0:T(8,128)(2,1)} %get-tuple-element.12), channel_id=1, source_target_pairs={{0,24},{2,0},{4,2},{6,4},{14,6},{8,14},{10,8},{12,10},{20,12},{22,... | collective-permute-start | bytes 6291464 | tf_op jit(solution)/shard_map/ppermute | solution.py:516
  501.4 23.7 %copy-start = (f32[128,8192]{1,0:T(8,128)S(1)}, f32[128,8192]{1,0:T(8,128)}, u32[]{:S(2)}) copy-start(f32[128,8192]{1,0:T(8,128)} %get-tuple-element.10.a) | copy-start | bytes 12582916

commit v4 on v3

--- a/solution.py
+++ b/solution.py
@@ -12,7 +12,8 @@
 F32, BF16 = jnp.float32, jnp.bfloat16
 SUB = 4
 TILE = 256
-VMEM_LIMIT = 63 * 2**20
+FILL = 512
+VMEM_LIMIT = 67043328
 
 
 def ring_pos(side, chip, ring):
@@ -48,13 +49,13 @@
     return p * cdf, slope
 
 
-def kernel(n, x, dy, pre, w_in, w_down, snd0, snd1, terms, dw_in, dw_down, gb, rsb, sbb, dpre, w2,
-           agr, ags, d2r, d2s, rsr, rss, sbr, sbs, wsem, psem, osem, lsem, tsem, fsem):
+def kernel(n, x, dy, pre, w_in, w_down, snd0, snd1, terms, filled, dw_in, dw_down, gb, rsb, sbb, dpre, w2, late,
+           agr, ags, d2r, d2s, rsr, rss, sbr, sbs, wsem, psem, osem, lsem, tsem, fsem, gsem, xsem):
     S = n // 2
     G = S // 2
     side = math.isqrt(S)
     R, D = x.shape
-    H, Q, F = R // 2, R // SUB, pre.shape[1]
+    H, F = R // 2, pre.shape[1]
     DC, FC = D // SUB, F // SUB
     NT = D // TILE
     me = lax.axis_index("tp")
@@ -66,52 +67,63 @@
     def remote(src, dst, ssem, rsem, dev):
         return pltpu.make_async_remote_copy(src, dst, ssem, rsem, device_id={"tp": dev}, device_id_type=MESH)
 
+    def arrived(ref, sem):
+        remote(ref, ref, rss.at[0, 0], sem, sib).wait_recv()
+
+    def left(ref, sem):
+        remote(ref, ref, sem, rsr.at[0, 0], sib).wait_send()
+
     def land(v, d):
         return S * (v // G) + jnp.where(v % G == G - 1, S - 2, 2 * (v % G) + d)
 
-    def ag_copy(v, d, q, src=None):
-        rows = pl.ds(q * Q if isinstance(q, int) else pl.multiple_of(q * Q, Q), Q)
+    def half_of(e, d):
+        q = (e + d) % 2
+        return pl.ds(q * H if isinstance(q, int) else pl.multiple_of(q * H, H), H)
+
+    def ag_copy(v, d, e, src=None):
+        rows = half_of(e, d)
         slot = S * (v // G) + jnp.where(v % G == 0, S - 1, 2 * (v % G - 1) + d)
         src = gb.at[0, slot, rows] if src is None else src.at[rows]
-        return remote(src, gb.at[0, land(v, d), rows], ags.at[v, d], agr.at[v, d, q], nxt[d])
-
-    def goes(v, d, q):
-        return (v % G < G - 1) | ((q >= SUB // 2) if d else (q < SUB // 2))
-
-    def d2d_part(w, q):
-        rows = pl.ds(pl.multiple_of(q * Q, Q), Q)
-        return remote(gb.at[0, w, rows], gb.at[1, w, rows], d2s.at[w], d2r.at[w], sib)
-
-    def d2d(w, src=None):
-        return remote(gb.at[0, w] if src is None else src, gb.at[1, w], d2s.at[w], d2r.at[w], sib)
-
-    def pump(v, q):
-        for d in range(2):
-            @pl.when(goes(v, d, q))
+        return remote(src, gb.at[0, land(v, d), rows], ags.at[v // (G // 2)], agr.at[v, e], nxt[d])
+
+    def handed(w):
+        return jnp.where(w < S - 2, w // 2, jnp.where(w < S, w - S // 2 + 1, S // 2 + 1 + (w - S) // (S // 2)))
+
+    def hand(w, rows=None, src=None):
+        ref = gb.at[0, w] if src is None else src
+        dst = gb.at[1, w]
+        if rows is not None:
+            ref, dst = ref.at[rows], dst.at[rows]
+        return remote(ref, dst, d2s.at[w // (S // 2)], d2r.at[handed(w)], sib)
+
+    def pump(v, e):
+        @pl.when((v % G < G - 1) | (e == 0))
+        def _():
+            arrived(gb.at[0, 0], agr.at[v, e])
+
+            @pl.when((v % G < G - 2) | ((v % G == G - 2) & (e == 0)))
             def _():
-                ag_copy(v, d, q).wait_recv()
-
-                @pl.when((v % G < G - 1) & goes(v + 1, d, q))
-                def _():
-                    ag_copy(v + 1, d, q).start()
-
-                d2d_part(land(v, d), q).start()
-
-        @pl.when((v == G - 2) & (q == SUB - 1))
-        def _():
-            for p in range(SUB):
                 for d in range(2):
-                    ag_copy(G, d, p).start()
+                    ag_copy(v + 1, d, e).start()
+
+            @pl.when((v == G - 2) & (e == 1))
+            def _():
+                for p in range(2):
+                    for d in range(2):
+                        ag_copy(G, d, p).start()
+
+            for d in range(2):
+                hand(land(v, d), half_of(e, d)).start()
 
     bar = pltpu.get_barrier_semaphore()
     for dev in (*nxt, sib):
         pl.semaphore_signal(bar, inc=1, device_id={"tp": dev}, device_id_type=MESH)
     pl.semaphore_wait(bar, 3)
-    for q in range(SUB):
+    for e in range(2):
         for d in range(2):
-            ag_copy(0, d, q, dy).start()
-    d2d(S - 1, dy).start()
-    d2d(2 * S - 1, x).start()
+            ag_copy(0, d, e, dy).start()
+    hand(S - 1, src=dy).start()
+    hand(2 * S - 1, src=x).start()
 
     def first(hT):
         def p1(w1, a, prb, wst):
@@ -136,15 +148,27 @@
                 away = jnp.where(e == S - 1, 0, jnp.where(e == S - 2, S // 2, jnp.where(e % 2 == 0, S - 1 - e // 2, e // 2 + 1)))
                 for h, (ps, cr) in enumerate(((pos, core), (pos2, 1 - core))):
                     row = pl.multiple_of((ring_chip(side, ps + away - S, cr) * 2 + cr) * R, R)
-                    out.append(pltpu.make_async_copy(pre.at[pl.ds(row, R)], prb.at[b, h], psem.at[b, h]))
+                    out.append(pltpu.make_async_copy(pre.at[pl.ds(row, R)], prb.at[b, h], psem.at[b]))
                 rows = pl.ds(pl.multiple_of(u * (D // S), D // S), D // S)
                 out.append(pltpu.make_async_copy(w_in.at[rows], wst, wsem.at[1]))
                 return out
 
             def fetch(u):
-                d2d(slot_of(u)).wait_recv()
+                @pl.when((u % 2 == 1) & (u < S - 1))
+                def _():
+                    arrived(gb.at[1, pl.ds(0, 2)], d2r.at[handed(slot_of(u))])
+
+                @pl.when((u == 0) | (u == S - 1))
+                def _():
+                    arrived(gb.at[1, 0], d2r.at[handed(slot_of(u))])
+
                 for c in loads(u):
                     c.start()
+
+            def fetched(u):
+                b = u % 2
+                for ref, sem in ((a.at[b], lsem.at[b]), (prb.at[b], psem.at[b]), (wst, wsem.at[1])):
+                    pltpu.make_async_copy(ref, ref, sem).wait()
 
             fetch(0)
             load_w1.wait()
@@ -158,9 +182,9 @@
 
                     @pl.loop(0, SUB)
                     def _(j):
-                        @pl.when(j % 2 == 0)
+                        @pl.when(j == 0)
                         def _():
-                            pump(v, half * (SUB // 2) + j // 2)
+                            pump(v, half)
 
                         @pl.when(busy)
                         def _():
@@ -168,9 +192,7 @@
 
                             @pl.when(j == 0)
                             def _():
-                                for c in loads(u):
-                                    c.wait()
-
+                                fetched(u)
                                 w2[:, pl.ds(pl.multiple_of(u * (D // S), D // S), D // S)] = wst[...].T
 
                                 @pl.when((half == 0) & (u + 1 < S))
@@ -202,16 +224,16 @@
                 return pltpu.make_async_copy(dout.at[i % 2], dw_down.at[:, cols], osem.at[i % 2])
 
             def sib_copy(k, c):
-                return remote(sst.at[k % 2, c], sbb.at[k, c], sbs.at[k % 2, c], sbr.at[k, c], sib)
+                return remote(sst.at[k % 2, c], sbb.at[k, c], sbs.at[k % 2], sbr.at[k], sib)
 
             tile_load(0).start()
 
             @pl.loop(0, S)
             def _(g):
                 def step(w):
-                    @pl.when(w % 2 == 0)
-                    def _():
-                        pump(G + 1 + w // (2 * SUB), (w // 2) % SUB)
+                    @pl.when(w % 4 == 3)
+                    def _():
+                        pump(G + 1 + w // 8, (w // 4) % 2)
 
                 step(3 * g)
 
@@ -219,9 +241,9 @@
                 def _(j):
                     k, c = G - 1 - g // 2, (g % 2) * 2 + j
 
-                    @pl.when(g >= 4)
-                    def _():
-                        sib_copy(k + 2, c).wait_send()
+                    @pl.when((g >= 4) & (c == 0))
+                    def _():
+                        left(sst.at[k % 2], sbs.at[k % 2])
 
                     part = dot(dpre[1, pl.ds(2 * k, 2)].reshape(2 * R, F), w2[:, pl.ds(pl.multiple_of(c * DC, DC), DC)], 1, 0)
                     sst[k % 2, c] = part.astype(BF16).reshape(2, R, DC)
@@ -248,29 +270,16 @@
                 tile_out(i).wait()
 
             for k in range(2):
-                for c in range(SUB):
-                    sib_copy(k, c).wait_send()
+                left(sst.at[k], sbs.at[k])
 
         pl.run_scoped(p2, pltpu.VMEM((2, 2, S, R, TILE), BF16), pltpu.VMEM((2, F, TILE), BF16), pltpu.VMEM((2, SUB, 2, R, DC), BF16))
 
     pl.run_scoped(first, pltpu.VMEM((F, 2 * S * R), BF16))
 
     def sent():
-        @pl.loop(0, 2 * G)
-        def _(v):
-            for d in range(2):
-                @pl.when(v % G < G - 1)
-                def _():
-                    remote(gb.at[0, 0], gb.at[0, 0], ags.at[v, d], agr.at[v, d, 0], nxt[d]).wait_send()
-
-                @pl.when(v % G == G - 1)
-                def _():
-                    half = gb.at[0, 0, pl.ds(0, H)]
-                    remote(half, half, ags.at[v, d], agr.at[v, d, 0], nxt[d]).wait_send()
-
-        @pl.loop(0, 2 * S)
-        def _(w):
-            d2d(w).wait_send()
+        for v in range(4):
+            left(gb.at[0, pl.ds(0, S // 2 - v % 2)], ags.at[v])
+            left(gb.at[0, pl.ds(0, S // 2)], d2s.at[v])
 
     def p3(own, xt, eo, got, gsib, out, tb):
         def x_load(i):
@@ -281,30 +290,43 @@
             return pltpu.make_async_copy(eo.at[i % 2], dw_in.at[pl.ds(pl.multiple_of(i * TILE, TILE), TILE)], osem.at[i % 2])
 
         def rs_copy(r, i, q):
-            return remote(out.at[r % 2, q, i], rsb.at[r, q, i], rss.at[r % 2, i, q], rsr.at[r, i, q], nxt[1 - i])
+            return remote(out.at[r % 2, q, i], rsb.at[r, q, i], rss.at[r % 2, q], rsr.at[r, q], nxt[1 - i])
+
+        def rs_late(i):
+            r, q = G - 2, SUB - 1
+            return remote(out.at[r % 2, q, i], late.at[i], rss.at[r % 2, q], rsr.at[r, q], nxt[1 - i])
+
+        def rs_fill(i):
+            return remote(out.at[(G - 1) % 2, 0, i, :, pl.ds(0, FILL)], filled.at[i], xsem.at[0], xsem.at[1], nxt[1 - i])
 
         def rs_half(i, q):
             rows = pl.ds(H * (1 - i), H)
-            return remote(out.at[0, q, 0, rows], rsb.at[0, q, i, rows], rss.at[0, i, q], rsr.at[0, i, q], nxt[1 - i])
+            return remote(out.at[0, q, 0, rows], rsb.at[0, q, i, rows], rss.at[0, q], rsr.at[0, q], nxt[1 - i])
 
         def got_load(r, i, q):
-            return pltpu.make_async_copy(rsb.at[r - 1, q, i], got.at[q % 2, i], fsem.at[2 + i, q])
+            return pltpu.make_async_copy(rsb.at[r - 1, q, i], got.at[q % 2, i], gsem.at[q % 2, i])
 
         def got_half(i, q):
             rows = pl.ds(H * (1 - i), H)
-            return pltpu.make_async_copy(rsb.at[0, q, i, rows], got.at[q % 2, i, rows], fsem.at[2 + i, q])
+            return pltpu.make_async_copy(rsb.at[0, q, i, rows], got.at[q % 2, i, rows], gsem.at[q % 2, i])
 
         def sib_load(r, q):
-            return pltpu.make_async_copy(sbb.at[G - 1 - r, q], gsib.at[q % 2], psem.at[0, q % 2])
+            return pltpu.make_async_copy(sbb.at[G - 1 - r, q], gsib.at[q % 2], psem.at[q % 2])
 
         def sib_arrive(r, q):
-            remote(sbb.at[G - 1 - r, q], sbb.at[G - 1 - r, q], sbs.at[0, q], sbr.at[G - 1 - r, q], sib).wait_recv()
+            @pl.when(q == 0)
+            def _():
+                arrived(sbb.at[G - 1 - r], sbr.at[G - 1 - r])
 
         def col(q):
             return pl.ds(pl.multiple_of(q * DC, DC), DC)
 
         def snd_out(i, q):
-            return pltpu.make_async_copy(out.at[(G - 1) % 2, q, i], (snd1, snd0)[i].at[:, col(q)], fsem.at[i, q])
+            if isinstance(q, int) and q == 0:
+                cols, to = pl.ds(FILL, DC - FILL), pl.ds(0, DC - FILL)
+            else:
+                cols, to = pl.ds(0, DC), pl.ds(pl.multiple_of(q * DC - FILL, FILL), DC)
+            return pltpu.make_async_copy(out.at[(G - 1) % 2, q, i, :, cols], (snd1, snd0)[i].at[:, to], fsem.at[i])
 
         def term_out(q):
             return pltpu.make_async_copy(tb.at[q % 2], terms.at[:, col(q)], wsem.at[1 + q % 2])
@@ -340,35 +362,58 @@
 
                     tb[q % 2] = own[1] + gsib[q % 2, 1].astype(F32)
                     term_out(q).start()
-                    pump(2 * G - 1, q)
+
+                    @pl.when(q == SUB - 1)
+                    def _():
+                        pump(2 * G - 1, 0)
 
                 @pl.when(r == 2)
                 def _():
-                    for i in range(2):
-                        rs_half(i, q).wait_send()
+                    left(out.at[0, q, 0], rss.at[0, q])
+
+                @pl.when(r > 2)
+                def _():
+                    left(out.at[r % 2, q], rss.at[r % 2, q])
+
+                @pl.when((r == G - 1) & (q == SUB - 1))
+                def _():
+                    arrived(late, rsr.at[G - 2, SUB - 1])
 
                 for i in range(2):
-                    @pl.when(r > 2)
-                    def _():
-                        rs_copy(r - 2, i, q).wait_send()
-
                     @pl.when(r == 1)
                     def _():
                         got_half(i, q).wait()
 
-                    @pl.when(r > 1)
+                    end = (r == G - 1) & (q == SUB - 1)
+
+                    @pl.when((r > 1) & jnp.logical_not(end))
                     def _():
                         got_load(r, i, q).wait()
 
-                    @pl.when(r > 0)
+                    @pl.when((r > 0) & jnp.logical_not(end))
                     def _():
                         out[r % 2, q, i] = (own[i] + gsib[q % 2, i].astype(F32) + got[q % 2, i].astype(F32)).astype(BF16)
 
-                    @pl.when((r > 0) & (r < G - 1))
+                    @pl.when(end)
+                    def _():
+                        out[r % 2, q, i] = (own[i] + gsib[q % 2, i].astype(F32) + late[i].astype(F32)).astype(BF16)
+
+                    to_late = (r == G - 2) & (q == SUB - 1)
+
+                    @pl.when((r > 0) & (r < G - 1) & jnp.logical_not(to_late))
                     def _():
                         rs_copy(r, i, q).start()
 
-                    @pl.when(r == G - 1)
+                    @pl.when(to_late)
+                    def _():
+                        rs_late(i).start()
+
+                    @pl.when((r == G - 1) & (q == 0))
+                    def _():
+                        rs_fill(i).start()
+                        snd_out(i, 0).start()
+
+                    @pl.when((r == G - 1) & (q > 0))
                     def _():
                         snd_out(i, q).start()
 
@@ -382,14 +427,14 @@
 
                     @pl.when(r1 == 1)
                     def _():
+                        arrived(rsb.at[0, 0, 0], rsr.at[0, q1])
                         for i in range(2):
-                            rs_half(i, q1).wait_recv()
                             got_half(i, q1).start()
 
-                    @pl.when(r1 > 1)
-                    def _():
+                    @pl.when((r1 > 1) & ((r1 < G - 1) | (q1 < SUB - 1)))
+                    def _():
+                        arrived(rsb.at[0, 0], rsr.at[r1 - 1, q1])
                         for i in range(2):
-                            rs_copy(r1 - 1, i, q1).wait_recv()
                             got_load(r1, i, q1).start()
 
                 extra = jnp.where(r < G - 1, 1, 0)
@@ -402,9 +447,8 @@
 
                     @pl.when(i == 0)
                     def _():
-                        @pl.loop(S, 2 * S)
-                        def _(w):
-                            d2d(w).wait_recv()
+                        for lot in range(2):
+                            arrived(gb.at[1, pl.ds(0, S // 2)], d2r.at[S // 2 + 1 + lot])
 
                         x_load(0).start()
 
@@ -428,12 +472,13 @@
         for i in range(NT - 2, NT):
             e_out(i).wait()
         for q in range(SUB):
-            for i in range(2):
-                rs_copy(G - 2, i, q).wait_send()
-            for i in range(2):
-                snd_out(i, q).wait()
+            left(out.at[0, q], rss.at[(G - 2) % 2, q])
         for q in range(SUB - 2, SUB):
             term_out(q).wait()
+        for i, snd in enumerate((snd1, snd0)):
+            pltpu.make_async_copy(snd, snd, fsem.at[i]).wait()
+        left(filled, xsem.at[0])
+        arrived(filled, xsem.at[1])
 
     pl.run_scoped(p3, pltpu.VMEM((2, R, DC), F32), pltpu.VMEM((2, 2, S, R, TILE), BF16), pltpu.VMEM((2, TILE, F), BF16),
                   pltpu.VMEM((2, 2, R, DC), BF16), pltpu.VMEM((2, 2, R, DC), BF16), pltpu.VMEM((2, SUB, 2, R, DC), BF16),
@@ -442,12 +487,13 @@
 
 def copy_kernel(a, b, a2, b2, abuf, bbuf, isem, osem):
     get, put = [], []
-    for src, dst, buf in ((a, a2, abuf), (b, b2, bbuf)):
-        parts, rows = buf.shape[:2]
-        for i in range(parts):
-            at = pl.ds(i * rows, rows)
-            get.append(pltpu.make_async_copy(src.at[at], buf.at[i], isem.at[len(get)]))
-            put.append(pltpu.make_async_copy(buf.at[i], dst.at[at], osem.at[len(put)]))
+    for src, dst, buf, sizes in ((a, a2, abuf, (4, 12, 16)), (b, b2, bbuf, (16, 12, 4))):
+        unit, row = src.shape[0] // sum(sizes), 0
+        for size in sizes:
+            at = pl.ds(row, size * unit)
+            row += size * unit
+            get.append(pltpu.make_async_copy(src.at[at], buf.at[at], isem.at[len(get)]))
+            put.append(pltpu.make_async_copy(buf.at[at], dst.at[at], osem.at[len(put)]))
     for c in get:
         c.start()
     for g, p in zip(get, put):
@@ -458,30 +504,44 @@
 
 
 def copied(a, b):
-    parts = 4
     dma = pltpu.SemaphoreType.DMA
     return pl.pallas_call(
         copy_kernel,
         out_shape=[jax.ShapeDtypeStruct(t.shape, t.dtype) for t in (a, b)],
         in_specs=[pl.BlockSpec(memory_space=pl.ANY)] * 2,
         out_specs=[pl.BlockSpec(memory_space=pl.ANY)] * 2,
-        scratch_shapes=[pltpu.VMEM((parts, t.shape[0] // parts, t.shape[1]), t.dtype) for t in (a, b)] + [dma((2 * parts,))] * 2,
+        scratch_shapes=[pltpu.VMEM(t.shape, t.dtype) for t in (a, b)] + [dma((6,))] * 2,
         compiler_params=pltpu.CompilerParams(vmem_limit_bytes=48 * 2**20),
         cost_estimate=pl.CostEstimate(flops=8 * 10**9, bytes_accessed=8 * a.size, transcendentals=0),
         name="copy_out",
     )(a, b)
 
 
-def add_kernel(a, b, c, o):
-    o[...] = (a[...] + b[...].astype(F32) + c[...].astype(F32)).astype(BF16)
-
-
-def added(term, ahead, back):
+def add_kernel(a, b, c, f, o, v, sem):
+    n, parts = f.shape[2], sem.shape[0]
+    wide = a.shape[1] // parts
+    out = []
+    for i in range(parts):
+        at = i * wide
+        if i == 0:
+            v[:, :n] = (a[:, :n] + f[1].astype(F32) + f[0].astype(F32)).astype(BF16)
+            at = n
+        cols, part = slice(at, (i + 1) * wide), slice(at - n, (i + 1) * wide - n)
+        v[:, cols] = (a[:, cols] + b[:, part].astype(F32) + c[:, part].astype(F32)).astype(BF16)
+        done = pl.ds(i * wide, wide)
+        out.append(pltpu.make_async_copy(v.at[:, done], o.at[:, done], sem.at[i]))
+        out[-1].start()
+    for copy in out:
+        copy.wait()
+
+
+def added(term, ahead, back, filled):
     whole = pl.BlockSpec(memory_space=pltpu.VMEM)
     return pl.pallas_call(
-        add_kernel, in_specs=[whole] * 3, out_specs=whole, out_shape=jax.ShapeDtypeStruct(term.shape, BF16), name="last_add",
+        add_kernel, in_specs=[whole] * 4, out_specs=pl.BlockSpec(memory_space=pl.ANY), out_shape=jax.ShapeDtypeStruct(term.shape, BF16),
+        scratch_shapes=[pltpu.VMEM(term.shape, BF16), pltpu.SemaphoreType.DMA((4,))], name="last_add",
         compiler_params=pltpu.CompilerParams(vmem_limit_bytes=16 * 2**20),
-    )(term, ahead, back)
+    )(term, ahead, back, filled)
 
 
 def solution(mesh):
@@ -495,26 +555,25 @@
         F = pre.shape[1]
         sds = jax.ShapeDtypeStruct
         dma = pltpu.SemaphoreType.DMA
-        *sums, term, dw_in, dw_down, _, _, _ = pl.pallas_call(
+        *sums, term, filled, dw_in, dw_down, _, _, _ = pl.pallas_call(
             functools.partial(kernel, n),
             out_shape=(
-                sds((R, D), BF16), sds((R, D), BF16), sds((R, D), F32), sds((D, F), BF16), sds((F, D), BF16),
+                sds((R, D - FILL), BF16), sds((R, D - FILL), BF16), sds((R, D), F32), sds((2, R, FILL), BF16), sds((D, F), BF16), sds((F, D), BF16),
                 sds((2, 2 * S, R, D), BF16), sds((G - 1, SUB, 2, R, D // SUB), BF16), sds((G, SUB, 2, R, D // SUB), BF16),
             ),
             in_specs=[pl.BlockSpec(memory_space=pl.ANY)] * 5,
-            out_specs=[pl.BlockSpec(memory_space=pl.ANY)] * 8,
+            out_specs=[pl.BlockSpec(memory_space=pl.ANY)] * 9,
             scratch_shapes=[
-                pltpu.VMEM((2, S, R, F), BF16), pltpu.VMEM((F, D), BF16),
-                dma((2 * G, 2, SUB)), dma((2 * G, 2)), dma((2 * S,)), dma((2 * S,)),
-                dma((G - 1, 2, SUB)), dma((2, 2, SUB)), dma((G, SUB)), dma((2, SUB)),
-                dma((3,)), dma((2, 2)), dma((2,)), dma((2,)), dma((2,)), dma((4, SUB)),
+                pltpu.VMEM((2, S, R, F), BF16), pltpu.VMEM((F, D), BF16), pltpu.VMEM((2, R, D // SUB), BF16),
+                dma((2 * G, 2)), dma((4,)), dma((G + 3,)), dma((4,)), dma((G - 1, SUB)), dma((2, SUB)), dma((G,)), dma((2,)),
+                dma((3,)), dma((2,)), dma((2,)), dma((2,)), dma((2,)), dma((2,)), dma((2, 2)), dma((2,)),
             ],
             compiler_params=pltpu.CompilerParams(collective_id=0, has_side_effects=True, vmem_limit_bytes=VMEM_LIMIT),
             name="mlp_backward",
         )(x, dy, pre, w_in, w_down)
         dw_in, dw_down = copied(dw_in, dw_down)
         ahead, back = (lax.ppermute(a, "tp", perm) for a, perm in zip(sums, perms))
-        return added(term, ahead, back), dw_in, dw_down
+        return added(term, ahead, back, filled), dw_in, dw_down
 
     rows, cols = P(("dp", "tp"), None), P("dp", "tp")
     return jax.shard_map(

time: 528 us -> 524 us (level)
  transfers between devices with their start and end apart: 2 -> 2, of which waited for: 1 -> 0; matrix products, arithmetic and copies ran while one was open for 0% -> 0% of each run, Pallas kernels for 4% -> 4%
where the time goes in v4:
time: 524 us
  Pallas kernels  519 us (99%)
    pallas_call x1, Pallas kernels, step(): pl.pallas_call(functools.partial(kernel, n), out_shape=(sds((R, D - FILL)...  495 us
    pallas_call x1, Pallas kernels, copied(): pl.pallas_call(copy_kernel, out_shape=[jax.ShapeDtypeStruct(t.shape, t.dt...  22.7 us
  transfers between devices with their start and end apart: 2, of which 0 were waited for; matrix products, arithmetic and copies ran while one was open for 0% of the time, Pallas kernels for 4%

profile of v4, /device:TPU:97, one launch (start us, length us, event | category | flops | bytes accessed | tf_op | source)
XLA Modules:
  0.0 523.7 jit_solution(5516339504572533646)
XLA Ops:
  0.6 495.1 %mlp_backward.1 = (bf16[128,7680]{1,0:T(8,128)(2,1)}, bf16[128,7680]{1,0:T(8,128)(2,1)}, f32[128,8192]{1,0:T(8,128)}, bf16[2,128,512]{2,1,0:T(8,128)(2,1)}, bf16...) custom-call(bf16[128,8192]{1,0:T(8,128)(2,1)} %x.1, ...), custom_call_target="tpu_custom_call" | custom-call | tf_op jit(solution)/shard_map/mlp_backward/pallas_call | solution.py:558
  495.7 0.1 collective-permute-start
  495.8 2.7 collective-permute-start.1
  498.5 0.0 copy-start
  498.5 0.0 copy-start.1
  498.5 22.7 %copy_out.1 = (bf16[8192,1024]{1,0:T(8,128)(2,1)}, bf16[1024,8192]{1,0:T(8,128)(2,1)}) custom-call(bf16[8192,1024]{1,0:T(8,128)(2,1)} %get-tuple-element.15.a, bf16[1024,8192]{1,0:T(8,128)(2,1)} %get-tuple-element.16.b), custom_call_target="tpu_custom_call" | custom-call | flops 8000000000 | bytes 67108864 | tf_op jit(solution)/shard_map/copy_out/pallas_call | solution.py:508
  521.2 0.0 collective-permute-done.b
  521.3 0.0 collective-permute-done.1.c
  521.3 0.9 copy-done
  522.1 0.0 copy-done.1
  522.2 1.5 last_add.1
Async XLA Ops:
  495.7 25.5 %collective-permute-start = (bf16[128,7680]{1,0:T(8,128)(2,1)}, bf16[128,7680]{1,0:T(8,128)(2,1)S(1)}, u32[]{:S(2)}, u32[]{:S(2)}) collective-permute-start(bf16[128,7680]{1,0:T(8,128)(2,1)} %get-tuple-element.12), channel_id=1, source_target_pairs={{0,2},{2,4},{4,6},{6,14},{14,8},{8,10},{10,12},{12,20},{20,22},{22... | collective-permute-start | bytes 5898248 | tf_op jit(solution)/shard_map/ppermute | solution.py:575
  495.8 25.4 %collective-permute-start.1 = (bf16[128,7680]{1,0:T(8,128)(2,1)}, bf16[128,7680]{1,0:T(8,128)(2,1)S(1)}, u32[]{:S(2)}, u32[]{:S(2)}) collective-permute-start(bf16[128,7680]{1,0:T(8,128)(2,1)} %get-tuple-element.13), channel_id=1, source_target_pairs={{0,24},{2,0},{4,2},{6,4},{14,6},{8,14},{10,8},{12,10},{20,12},{22,... | collective-permute-start | bytes 5898248 | tf_op jit(solution)/shard_map/ppermute | solution.py:575
  498.5 23.6 %copy-start = (f32[128,8192]{1,0:T(8,128)S(1)}, f32[128,8192]{1,0:T(8,128)}, u32[]{:S(2)}) copy-start(f32[128,8192]{1,0:T(8,128)} %get-tuple-element.11.a) | copy-start | bytes 12582916
  498.5 23.7 %copy-start.1 = (bf16[2,128,512]{2,1,0:T(8,128)(2,1)S(1)}, bf16[2,128,512]{2,1,0:T(8,128)(2,1)}, u32[]{:S(2)}) copy-start(bf16[2,128,512]{2,1,0:T(8,128)(2,1)} %get-tuple-element.14.f) | copy-start | bytes 786436

commit v5 on v4

--- a/solution.py
+++ b/solution.py
@@ -45,7 +45,7 @@
     sq = p * p
     t = jnp.tanh(c * (p + 0.044715 * (sq * p)))
     cdf = 0.5 * (1.0 + t)
-    slope = cdf + p * (0.5 * (1.0 - t * t)) * (c * (1.0 + 3 * 0.044715 * sq))
+    slope = cdf + p * (cdf * (1.0 - t)) * (c * (1.0 + 3 * 0.044715 * sq))
     return p * cdf, slope
 
 
@@ -487,7 +487,7 @@
 
 def copy_kernel(a, b, a2, b2, abuf, bbuf, isem, osem):
     get, put = [], []
-    for src, dst, buf, sizes in ((a, a2, abuf, (4, 12, 16)), (b, b2, bbuf, (16, 12, 4))):
+    for src, dst, buf, sizes in ((a, a2, abuf, (4, 12, 16)), (b, b2, bbuf, (12, 12, 8))):
         unit, row = src.shape[0] // sum(sizes), 0
         for size in sizes:
             at = pl.ds(row, size * unit)

time: 524 us -> 524 us (level)
  no operation moved by 1% of the time
where the time goes in v5:
time: 524 us; the launch traced here: 523 us
  Pallas kernels  519 us (99%)
    pallas_call x1, Pallas kernels, step(): pl.pallas_call(functools.partial(kernel, n), out_shape=(sds((R, D - FILL)...  495 us
    pallas_call x1, Pallas kernels, copied(): pl.pallas_call(copy_kernel, out_shape=[jax.ShapeDtypeStruct(t.shape, t.dt...  22.8 us
  transfers between devices with their start and end apart: 2, of which 0 were waited for; matrix products, arithmetic and copies ran while one was open for 0% of the time, Pallas kernels for 4%

profile of v5, /device:TPU:97, one launch (start us, length us, event | category | flops | bytes accessed | tf_op | source)
XLA Modules:
  0.0 523.3 jit_solution(15061188109115153027)
XLA Ops:
  0.6 495.1 %mlp_backward.1 = (bf16[128,7680]{1,0:T(8,128)(2,1)}, bf16[128,7680]{1,0:T(8,128)(2,1)}, f32[128,8192]{1,0:T(8,128)}, bf16[2,128,512]{2,1,0:T(8,128)(2,1)}, bf16...) custom-call(bf16[128,8192]{1,0:T(8,128)(2,1)} %x.1, ...), custom_call_target="tpu_custom_call" | custom-call | tf_op jit(solution)/shard_map/mlp_backward/pallas_call | solution.py:558
  495.7 0.1 collective-permute-start
  495.8 2.7 collective-permute-start.1
  498.5 0.0 copy-start
  498.5 0.0 copy-start.1
  498.5 22.8 %copy_out.1 = (bf16[8192,1024]{1,0:T(8,128)(2,1)}, bf16[1024,8192]{1,0:T(8,128)(2,1)}) custom-call(bf16[8192,1024]{1,0:T(8,128)(2,1)} %get-tuple-element.15.a, bf16[1024,8192]{1,0:T(8,128)(2,1)} %get-tuple-element.16.b), custom_call_target="tpu_custom_call" | custom-call | flops 8000000000 | bytes 67108864 | tf_op jit(solution)/shard_map/copy_out/pallas_call | solution.py:508
  521.3 0.0 collective-permute-done.b
  521.3 0.0 collective-permute-done.1.c
  521.3 0.2 copy-done
  521.6 0.2 copy-done.1
  521.8 1.5 last_add.1
Async XLA Ops:
  495.7 25.6 %collective-permute-start = (bf16[128,7680]{1,0:T(8,128)(2,1)}, bf16[128,7680]{1,0:T(8,128)(2,1)S(1)}, u32[]{:S(2)}, u32[]{:S(2)}) collective-permute-start(bf16[128,7680]{1,0:T(8,128)(2,1)} %get-tuple-element.12), channel_id=1, source_target_pairs={{0,2},{2,4},{4,6},{6,14},{14,8},{8,10},{10,12},{12,20},{20,22},{22... | collective-permute-start | bytes 5898248 | tf_op jit(solution)/shard_map/ppermute | solution.py:575
  495.8 25.5 %collective-permute-start.1 = (bf16[128,7680]{1,0:T(8,128)(2,1)}, bf16[128,7680]{1,0:T(8,128)(2,1)S(1)}, u32[]{:S(2)}, u32[]{:S(2)}) collective-permute-start(bf16[128,7680]{1,0:T(8,128)(2,1)} %get-tuple-element.13), channel_id=1, source_target_pairs={{0,24},{2,0},{4,2},{6,4},{14,6},{8,14},{10,8},{12,10},{20,12},{22,... | collective-permute-start | bytes 5898248 | tf_op jit(solution)/shard_map/ppermute | solution.py:575
  498.5 23.1 %copy-start = (f32[128,8192]{1,0:T(8,128)S(1)}, f32[128,8192]{1,0:T(8,128)}, u32[]{:S(2)}) copy-start(f32[128,8192]{1,0:T(8,128)} %get-tuple-element.11.a) | copy-start | bytes 12582916
  498.5 23.3 %copy-start.1 = (bf16[2,128,512]{2,1,0:T(8,128)(2,1)S(1)}, bf16[2,128,512]{2,1,0:T(8,128)(2,1)}, u32[]{:S(2)}) copy-start(bf16[2,128,512]{2,1,0:T(8,128)(2,1)} %get-tuple-element.14.f) | copy-start | bytes 786436
